TPU v7x, 128 devices: a whole 4x4x4 slice. The times are simulated.
128 devices in a mesh: gx: 8 (over z, core), gy: 16 (over x, y).
Axes of the slice: x: 4, y: 4, z: 4, core: 2. Of those that a mesh axis runs over, the one named last changes fastest.
Arguments:
- table: float32 [1048576, 128], P(('gx', 'gy')), may hold values from -6 to 6
- accum: float32 [1048576], P(('gx', 'gy')), may hold values from 0.05 to 1
- cache_values: float32 [524288, 128], P(('gx', 'gy')), may hold values from -6 to 6
- cache_rows: int32 [524288], P(('gx', 'gy')), may hold values from 0 to 1048575, as said below
- pending: float32 [524288, 128], P(('gx', 'gy')), may hold values from -3 to 3
- batch_slots: int32 [3, 65536, 16], P(None, ('gx', 'gy')), may hold values from 0 to 4095
- targets: float32 [3, 65536, 128], P(None, ('gx', 'gy')), may hold values from -6 to 6
- dirty: int32 [3, 65536], P(None, ('gx', 'gy')), may hold values from 0 to 4095, as said below
Outputs:
- new_table: float32 [1048576, 128], P(('gx', 'gy'))
- new_accum: float32 [1048576], P(('gx', 'gy'))
- new_cache: float32 [524288, 128], P(('gx', 'gy'))
- new_pending: float32 [524288, 128], P(('gx', 'gy'))
Inputs may be any that keep to these rules, and one draw needn't show every extreme that they name: `cache_rows`: each device's slots form 128 blocks of 32 consecutive slots; every block holds rows of one owner, and every owner has exactly one block on every device. `dirty`: in each step a device's 512 entries are distinct slots of that device; at most 8 of them hold rows of one owner, and in every step some owner gets exactly 8 from every device.
All inputs are finite; a program needn't handle non-finite values.
Results may differ from a plain program's by a relative error of at most 0.0001.
Values sent between devices are 32-bit elements; how exact they have to be, the bound alone decides.
A program may use at most 128 MiB of HBM per device.

v0:
```python
import jax
import jax.numpy as jnp
from jax import lax
from jax.sharding import PartitionSpec as P

LEARN_RATE = 0.3


def cut_along(x, dim, count):
    shape = x.shape
    blocks = x.reshape(*shape[:dim], count, shape[dim] // count, *shape[dim + 1 :])
    return jnp.moveaxis(blocks, dim, 0)


def laid_out(blocks, dim):
    blocks = jnp.moveaxis(blocks, 0, dim)
    shape = blocks.shape
    return blocks.reshape(*shape[:dim], shape[dim] * shape[dim + 1], *shape[dim + 2 :])


def exchange_both(x, axis, axes, splits, concats):
    sizes = [lax.axis_size(a) for a in axes]
    blocks = cut_along(x, splits[0], sizes[0])
    blocks = jnp.moveaxis(cut_along(blocks, splits[1] + 1, sizes[1]), 0, 1)
    inside = blocks.shape[2:]
    blocks = blocks.reshape(-1, *inside)
    blocks = lax.all_to_all(blocks, axis, split_axis=0, concat_axis=0, tiled=True)
    blocks = laid_out(blocks.reshape(*sizes, *inside), concats[0] + 1)
    return laid_out(blocks, concats[1])


def body(table, accum, cache_values, cache_rows, pending, batch_slots, targets, dirty):
    devices = lax.axis_size(("gx", "gy"))
    span_x = lax.axis_size("gx")
    span_y = lax.axis_size("gy")
    rows_dev = table.shape[0]
    slots_dev = cache_values.shape[0]
    width = cache_values.shape[1]
    capacity = 2 * dirty.shape[1] // devices
    lookups = batch_slots.shape[2]
    for step in range(batch_slots.shape[0]):
        picks = batch_slots[step]
        pooled = jnp.mean(jnp.take(cache_values, picks, axis=0), axis=1)
        bag_grad = (pooled - targets[step]) / lookups
        spread = jnp.broadcast_to(bag_grad[:, None, :], (picks.shape[0], lookups, width)).reshape(
            -1, width
        )
        pending = pending + jax.ops.segment_sum(spread, picks.reshape(-1), num_segments=slots_dev)
        listed = dirty[step]
        flushed = jnp.take(pending, listed, axis=0)
        global_rows = jnp.take(cache_rows, listed)
        owner = global_rows // rows_dev
        local_rows = global_rows - owner * rows_dev
        order_ids = jnp.arange(listed.shape[0], dtype=jnp.int32)
        earlier = (owner[:, None] == owner[None, :]) & (order_ids[:, None] > order_ids[None, :])
        position = jnp.sum(earlier.astype(jnp.int32), axis=1)
        target_slot = owner * capacity + position
        outgoing = jnp.zeros((devices * capacity, width), jnp.float32).at[target_slot].set(flushed)
        out_index = (
            jnp.full((devices * capacity,), rows_dev, jnp.int32).at[target_slot].set(local_rows)
        )
        pending = pending.at[listed].set(0.0)
        got_values, got_index = (
            exchange_both(
                outgoing.reshape(span_x, span_y, capacity, width),
                ("gx", "gy"),
                ("gx", "gy"),
                (0, 1),
                (0, 1),
            ),
            exchange_both(
                out_index.reshape(span_x, span_y, capacity),
                ("gx", "gy"),
                ("gx", "gy"),
                (0, 1),
                (0, 1),
            ),
        )
        got_values = got_values.reshape(-1, width)
        got_index = got_index.reshape(-1)
        safe_index = jnp.minimum(got_index, rows_dev - 1)
        row_total = jax.ops.segment_sum(got_values, got_index, num_segments=rows_dev + 1)
        row_grad = jnp.take(row_total, got_index, axis=0)
        old_rows = jnp.take(table, safe_index, axis=0)
        old_accum = jnp.take(accum, safe_index)
        fresh_accum = old_accum + jnp.mean(row_grad * row_grad, axis=1)
        answer = old_rows - LEARN_RATE * row_grad / jnp.sqrt(fresh_accum)[:, None]
        table = table.at[got_index].set(answer, mode="drop")
        accum = accum.at[got_index].set(fresh_accum, mode="drop")
        returned = exchange_both(
            answer.reshape(span_x, span_y, capacity, width),
            ("gx", "gy"),
            ("gx", "gy"),
            (0, 1),
            (0, 1),
        )
        fresh = jnp.take(returned.reshape(-1, width), target_slot, axis=0)
        cache_values = cache_values.at[listed].set(fresh)
    return (table, accum, cache_values, pending)


def solution(mesh):
    in_specs = (
        P(("gx", "gy"), None),
        P(("gx", "gy")),
        P(("gx", "gy"), None),
        P(("gx", "gy")),
        P(("gx", "gy"), None),
        P(None, ("gx", "gy"), None),
        P(None, ("gx", "gy"), None),
        P(None, ("gx", "gy")),
    )
    out_specs = (
        P(("gx", "gy"), None),
        P(("gx", "gy")),
        P(("gx", "gy"), None),
        P(("gx", "gy"), None),
    )
    return jax.shard_map(body, mesh=mesh, in_specs=in_specs, out_specs=out_specs, check_vma=False)
```

profile of v0, /device:TPU:1, one launch (start us, length us, event | category | flops | bytes accessed | tf_op | source)
XLA Modules:
  0.0 547.9 jit_solution(371420204287840133)
XLA Ops:
  6.3 3.1 gather_fusion
  13.5 11.5 %all-to-all-start = ((s32[128,1,1,8]{3,2,1,0:T(1,128)}), s32[128,1,1,8]{3,2,1,0:T(1,128)S(1)}, u32[]{:S(2)}, u32[]{:S(2)}) async-start(s32[128,1,1,8]{3,2,1,0:T(1,128)} %bitcast.1), calls=%async_computation | async-start | bytes 131072 | tf_op jit(solution)/shard_map/all_to_all | solution.py:27
  27.3 3.1 gather_fusion.5
  31.2 3.1 gather_fusion.10
  34.9 27.7 %gather_fusion.2 = f32[8192,128]{1,0:T(8,128)} fusion(f32[4096,128]{1,0:T(8,128)S(1)} %copy.75, s32[8192]{0:T(1024)S(1)} %broadcast_clamp_fusion.2), kind=kCustom, calls=%fused_computation.2.clone | custom fusion | bytes 8421376 | tf_op jit(solution)/shard_map/jit(_take)/gather | solution.py:43
  62.6 5.3 select_reduce_fusion.2
  76.0 45.1 %scatter_fusion = f32[4096,128]{1,0:T(8,128)S(1)} fusion(f32[4096,128]{1,0:T(8,128)S(1)} %copy-done.4, s32[8192]{0:T(1024)S(1)} %reshape.509, f32[8192,128]{1,0:T(8,128)} %bitcast.171), kind=kCustom, calls=%fused_computation.22 | custom fusion | flops 1048576 | bytes 12615680 | tf_op jit(solution)/shard_map/scatter-add | solution.py:48
  121.1 3.6 scatter_custom_fusion.2
  124.7 2.7 scatter_custom_fusion.6
  127.4 9.8 %all-to-all-start.1 = ((f32[128,1,1,8,128]{4,3,2,1,0:T(8,128)}), f32[128,1,1,8,128]{4,3,2,1,0:T(8,128)S(1)}, u32[]{:S(2)}, u32[]{:S(2)}) async-start(f32[128,1,1,8,128]{4,3,2,1,0:T(8,128)} %bitcast.14), calls=%async_computation.1 | async-start | bytes 1048576 | tf_op jit(solution)/shard_map/all_to_all | solution.py:27
  137.5 5.0 gather_fusion.1
  142.5 6.2 %gather_fusion.4 = f32[1024]{0:T(1024)S(1)} fusion(f32[8192]{0:T(1024)S(1)} %copy.74, s32[1024]{0:T(1024)S(1)} %get-tuple-element.55), kind=kCustom, calls=%fused_computation.5.clone | custom fusion | bytes 12288 | tf_op jit(solution)/shard_map/jit(_take)/gather | solution.py:85
  150.5 8.0 %all-to-all-start.2 = ((s32[128,1,1,8]{3,2,1,0:T(1,128)}), s32[128,1,1,8]{3,2,1,0:T(1,128)S(1)}, u32[]{:S(2)}, u32[]{:S(2)}) async-start(s32[128,1,1,8]{3,2,1,0:T(1,128)} %bitcast.21), calls=%async_computation.2 | async-start | bytes 131072 | tf_op jit(solution)/shard_map/all_to_all | solution.py:27
  158.5 9.0 %scatter_custom_fusion.3 = f32[8193,128]{1,0:T(8,128)} fusion(s32[1024]{0:T(1024)S(1)} %reshape_reshape.34, f32[]{:T(128)} %constant.129.clone.1, f32[128,1,1,8,128]{4,3,2,1,0:T(8,128)S(1)} %all-to-all-done.1), kind=kCustom, calls=%fused_computation.52 | custom fusion | flops 131072 | bytes 4719108 | tf_op jit(solution)/shard_map/scatter-add | solution.py:82
  167.5 5.0 gather_fusion.3
  174.5 10.0 %all-to-all-start.3 = ((f32[128,1,1,8,128]{4,3,2,1,0:T(8,128)}), f32[128,1,1,8,128]{4,3,2,1,0:T(8,128)}, u32[]{:S(2)}, u32[]{:S(2)}) async-start(f32[128,1,1,8,128]{4,3,2,1,0:T(8,128)} %fusion.81), calls=%async_computation.3 | async-start | bytes 1048576 | tf_op jit(solution)/shard_map/all_to_all | solution.py:27
  188.4 9.1 %all-to-all-done.3 = f32[128,1,1,8,128]{4,3,2,1,0:T(8,128)} async-done(((f32[128,1,1,8,128]{4,3,2,1,0:T(8,128)}), f32[128,1,1,8,128]{4,3,2,1,0:T(8,128)}, u32[]{:S(2)}, u32[]{:S(2)}) %all-to-all-start.3) | async-done | bytes 524320 | tf_op jit(solution)/shard_map/all_to_all | solution.py:27
  197.5 7.7 %scatter_custom_fusion.7 = f32[4096,128]{1,0:T(8,128)} fusion(f32[4096,128]{1,0:T(8,128)} %copy-done.5, s32[512]{0:T(512)} %bitcast.199, f32[]{:T(128)} %constant.58.clone.3, pred[512]{0:T(512)(128)(4,1)S(1)} %copy-done.25, f32[1024,128]{1,0:T(8,128)} %bitcast.39, s32[1024]{0:T(1024)S(1)} %pad_clamp_fusion.3), kind=kCustom, calls=%fused_computation.84 | custom fusion | flops 65536 | bytes 2626560 | tf_op jit(solution)/shard_map/scatter | solution.py:98
  205.1 29.3 %gather_fusion.7 = f32[8192,128]{1,0:T(8,128)} fusion(f32[4096,128]{1,0:T(8,128)} %scatter_custom_fusion.7, s32[8192]{0:T(1024)S(1)} %broadcast_clamp_fusion.1), kind=kCustom, calls=%fused_computation.11.clone | custom fusion | bytes 8421376 | tf_op jit(solution)/shard_map/jit(_take)/gather | solution.py:43
  234.4 5.3 select_reduce_fusion.1
  242.9 45.5 %scatter_fusion.1 = f32[4096,128]{1,0:T(8,128)S(1)} fusion(f32[4096,128]{1,0:T(8,128)S(1)} %scatter_custom_fusion.6, s32[8192]{0:T(1024)S(1)} %reshape.565, f32[8192,128]{1,0:T(8,128)} %bitcast.172), kind=kCustom, calls=%fused_computation.29 | custom fusion | flops 1048576 | bytes 12615680 | tf_op jit(solution)/shard_map/scatter-add | solution.py:48
  288.5 3.6 scatter_custom_fusion.9
  292.1 5.8 %all-to-all-start.4 = ((f32[128,1,1,8,128]{4,3,2,1,0:T(8,128)}), f32[128,1,1,8,128]{4,3,2,1,0:T(8,128)}, u32[]{:S(2)}, u32[]{:S(2)}) async-start(f32[128,1,1,8,128]{4,3,2,1,0:T(8,128)} %bitcast.174), calls=%async_computation.4 | async-start | bytes 1048576 | tf_op jit(solution)/shard_map/all_to_all | solution.py:27
  298.0 8.1 %scatter_custom_fusion.4 = f32[8192,128]{1,0:T(8,128)} fusion(f32[8192,128]{1,0:T(8,128)} %copy.73, s32[1024]{0:T(1024)S(1)} %bitcast.190, f32[1024,128]{1,0:T(8,128)S(1)} %gather_fusion.1, f32[1024,128]{1,0:T(8,128)S(1)} %gather_fusion.3, f32[1024]{0:T(1024)S(1)} %get-tuple-element.29, pred[1024]{0:T(1024)(128)(4,1)S(1)} %compare_and_fusion.7, ...), kind=kCustom, calls=%fused_computation.212 | custom fusion | flops 655360 | bytes 5249024 | tf_op jit(solution)/shard_map/scatter | solution.py:88
  306.1 4.4 scatter_fusion.2
  310.5 5.0 gather_fusion.6
  315.5 6.2 %gather_fusion.9 = f32[1024]{0:T(1024)S(1)} fusion(f32[8192]{0:T(1024)S(1)} %scatter_fusion.2, s32[1024]{0:T(1024)S(1)} %get-tuple-element.53), kind=kCustom, calls=%fused_computation.17.clone | custom fusion | bytes 12288 | tf_op jit(solution)/shard_map/jit(_take)/gather | solution.py:85
  321.7 9.9 %all-to-all-start.5 = ((s32[128,1,1,8]{3,2,1,0:T(1,128)}), s32[128,1,1,8]{3,2,1,0:T(1,128)S(1)}, u32[]{:S(2)}, u32[]{:S(2)}) async-start(s32[128,1,1,8]{3,2,1,0:T(1,128)} %bitcast.50), calls=%async_computation.5 | async-start | bytes 131072 | tf_op jit(solution)/shard_map/all_to_all | solution.py:27
  331.6 8.2 %scatter_custom_fusion.10 = f32[8193,128]{1,0:T(8,128)} fusion(s32[1024]{0:T(1024)S(1)} %reshape_reshape.37, f32[]{:T(128)} %constant.129.clone.1, f32[128,1,1,8,128]{4,3,2,1,0:T(8,128)} %all-to-all-done.4), kind=kCustom, calls=%fused_computation.50 | custom fusion | flops 131072 | bytes 4719108 | tf_op jit(solution)/shard_map/scatter-add | solution.py:82
  339.8 5.0 gather_fusion.8
  347.4 12.1 %all-to-all-start.6 = ((f32[128,1,1,8,128]{4,3,2,1,0:T(8,128)}), f32[128,1,1,8,128]{4,3,2,1,0:T(8,128)}, u32[]{:S(2)}, u32[]{:S(2)}) async-start(f32[128,1,1,8,128]{4,3,2,1,0:T(8,128)} %fusion.79), calls=%async_computation.6 | async-start | bytes 1048576 | tf_op jit(solution)/shard_map/all_to_all | solution.py:27
  367.2 5.3 all-to-all-done.6
  372.5 7.7 %scatter_custom_fusion.15 = f32[4096,128]{1,0:T(8,128)} fusion(f32[4096,128]{1,0:T(8,128)} %scatter_custom_fusion.7, s32[512]{0:T(512)} %bitcast.197, f32[]{:T(128)} %constant.58.clone.3, pred[512]{0:T(512)(128)(4,1)} %get-tuple-element.16, f32[1024,128]{1,0:T(8,128)} %bitcast.68, s32[1024]{0:T(1024)S(1)} %pad_clamp_fusion.1), kind=kCustom, calls=%fused_computation.80 | custom fusion | flops 65536 | bytes 2626560 | tf_op jit(solution)/shard_map/scatter | solution.py:98
  380.2 29.3 %gather_fusion.12 = f32[8192,128]{1,0:T(8,128)} fusion(f32[4096,128]{1,0:T(8,128)} %scatter_custom_fusion.15, s32[8192]{0:T(1024)S(1)} %broadcast_clamp_fusion), kind=kCustom, calls=%fused_computation.12.clone | custom fusion | bytes 8421376 | tf_op jit(solution)/shard_map/jit(_take)/gather | solution.py:43
  409.5 5.3 select_reduce_fusion
  418.1 45.1 %scatter_fusion.3 = f32[4096,128]{1,0:T(8,128)S(1)} fusion(f32[4096,128]{1,0:T(8,128)S(1)} %scatter_custom_fusion.14, s32[8192]{0:T(1024)S(1)} %reshape.629, f32[8192,128]{1,0:T(8,128)} %bitcast.173), kind=kCustom, calls=%fused_computation.37 | custom fusion | flops 1048576 | bytes 12615680 | tf_op jit(solution)/shard_map/scatter-add | solution.py:48
  463.2 3.6 scatter_custom_fusion.17
  466.8 6.2 %all-to-all-start.7 = ((f32[128,1,1,8,128]{4,3,2,1,0:T(8,128)}), f32[128,1,1,8,128]{4,3,2,1,0:T(8,128)}, u32[]{:S(2)}, u32[]{:S(2)}) async-start(f32[128,1,1,8,128]{4,3,2,1,0:T(8,128)} %bitcast.175), calls=%async_computation.7 | async-start | bytes 1048576 | tf_op jit(solution)/shard_map/all_to_all | solution.py:27
  473.1 8.1 %scatter_custom_fusion.12 = f32[8192,128]{1,0:T(8,128)} fusion(f32[8192,128]{1,0:T(8,128)} %scatter_custom_fusion.4, s32[1024]{0:T(1024)S(1)} %bitcast.192, f32[1024,128]{1,0:T(8,128)S(1)} %gather_fusion.6, f32[1024,128]{1,0:T(8,128)S(1)} %gather_fusion.8, f32[1024]{0:T(1024)S(1)} %get-tuple-element.21, pred[1024]{0:T(1024)(128)(4,1)S(1)} %copy-done.18, ...), kind=kCustom, calls=%fused_computation.210 | custom fusion | flops 655360 | bytes 5249024 | tf_op jit(solution)/shard_map/scatter | solution.py:88
  481.2 4.4 scatter_fusion.4
  485.6 5.0 gather_fusion.11
  490.6 6.2 %gather_fusion.14 = f32[1024]{0:T(1024)S(1)} fusion(f32[8192]{0:T(1024)S(1)} %scatter_fusion.4, s32[1024]{0:T(1024)S(1)} %get-tuple-element.51), kind=kCustom, calls=%fused_computation.18.clone | custom fusion | bytes 12288 | tf_op jit(solution)/shard_map/jit(_take)/gather | solution.py:85
  496.8 9.3 %scatter_custom_fusion.18 = f32[8193,128]{1,0:T(8,128)} fusion(s32[1024]{0:T(1024)S(1)} %reshape_reshape.41, f32[]{:T(128)} %constant.129.clone.1, f32[128,1,1,8,128]{4,3,2,1,0:T(8,128)} %all-to-all-done.7), kind=kCustom, calls=%fused_computation.48 | custom fusion | flops 131072 | bytes 4719108 | tf_op jit(solution)/shard_map/scatter-add | solution.py:82
  506.1 5.0 gather_fusion.13
  513.2 10.2 %all-to-all-start.8 = ((f32[128,1,1,8,128]{4,3,2,1,0:T(8,128)}), f32[128,1,1,8,128]{4,3,2,1,0:T(8,128)}, u32[]{:S(2)}, u32[]{:S(2)}) async-start(f32[128,1,1,8,128]{4,3,2,1,0:T(8,128)} %fusion.77), calls=%async_computation.8 | async-start | bytes 1048576 | tf_op jit(solution)/shard_map/all_to_all | solution.py:27
  526.2 8.8 %scatter_custom_fusion.20 = f32[8192,128]{1,0:T(8,128)} fusion(f32[8192,128]{1,0:T(8,128)} %scatter_custom_fusion.12, s32[1024]{0:T(1024)S(1)} %bitcast.188, f32[1024,128]{1,0:T(8,128)S(1)} %gather_fusion.11, f32[1024,128]{1,0:T(8,128)S(1)} %gather_fusion.13, f32[1024]{0:T(1024)S(1)} %get-tuple-element.12, pred[1024]{0:T(1024)(128)(4,1)S(1)} %compare_and_fusion.3, ...), kind=kCustom, calls=%fused_computation.208 | custom fusion | flops 655360 | bytes 5249024 | tf_op jit(solution)/shard_map/scatter | solution.py:88
  535.1 4.6 scatter_fusion.5
  539.7 7.7 %scatter_custom_fusion.22 = f32[4096,128]{1,0:T(8,128)} fusion(f32[4096,128]{1,0:T(8,128)} %scatter_custom_fusion.15, s32[512]{0:T(512)} %bitcast.195, f32[]{:T(128)} %constant.58.clone.3, pred[512]{0:T(512)(128)(4,1)S(1)} %copy-done.24, f32[1024,128]{1,0:T(8,128)} %bitcast.86, s32[1024]{0:T(1024)S(1)} %pad_clamp_fusion), kind=kCustom, calls=%fused_computation.76 | custom fusion | flops 65536 | bytes 2626560 | tf_op jit(solution)/shard_map/scatter | solution.py:98
  (147 shorter events, 50.9 us)
Async XLA Ops:
  0.6 5.6 %copy-start = (s32[4096]{0:T(1024)S(1)}, s32[4096]{0:T(1024)}, u32[]{:S(2)}) copy-start(s32[4096]{0:T(1024)} %param.25) | copy-start | bytes 49156
  0.6 2.8 copy-start.6
  3.5 31.5 %copy-start.5 = (f32[4096,128]{1,0:T(8,128)}, f32[4096,128]{1,0:T(8,128)S(1)}, u32[]{:S(2)}) copy-start(f32[4096,128]{1,0:T(8,128)S(1)} %copy.75) | copy-start | bytes 6291460
  3.5 2.0 copy-start.11
  5.5 0.7 copy-start.15
  5.5 19.5 %copy-start.7 = (s32[3,512,16]{1,2,0:T(8,128)S(1)}, s32[3,512,16]{1,2,0:T(8,128)}, u32[]{:S(2)}) copy-start(s32[3,512,16]{1,2,0:T(8,128)} %param.27) | copy-start | bytes 294916
  13.5 113.9 %all-to-all-start = ((s32[128,1,1,8]{3,2,1,0:T(1,128)}), s32[128,1,1,8]{3,2,1,0:T(1,128)S(1)}, u32[]{:S(2)}, u32[]{:S(2)}) async-start(s32[128,1,1,8]{3,2,1,0:T(1,128)} %bitcast.1), calls=%async_computation | async-start | bytes 131072 | tf_op jit(solution)/shard_map/all_to_all | solution.py:27
  26.8 97.8 %copy-start.26 = (s32[512,1]{0,1:T(1,128)}, s32[512,1]{0,1:T(1,128)S(1)}, u32[]{:S(2)}) copy-start(s32[512,1]{0,1:T(1,128)S(1)} %get-tuple-element.45) | copy-start | bytes 6148
  31.2 31.4 %copy-start.13 = (s32[1024]{0:T(1024)}, s32[1024]{0:T(1024)S(1)}, u32[]{:S(2)}) copy-start(s32[1024]{0:T(1024)S(1)} %pad_clamp_fusion.2) | copy-start | bytes 12292
  68.0 8.0 %copy-start.4 = (f32[4096,128]{1,0:T(8,128)S(1)}, f32[4096,128]{1,0:T(8,128)}, u32[]{:S(2)}) copy-start(f32[4096,128]{1,0:T(8,128)} %param.26) | copy-start | bytes 6291460
  69.6 218.8 %copy-start.21 = (s32[512]{0:T(512)}, s32[512]{0:T(512)S(1)}, u32[]{:S(2)}) copy-start(s32[512]{0:T(512)S(1)} %get-tuple-element.17) | copy-start | bytes 6148
  127.4 23.1 %all-to-all-start.1 = ((f32[128,1,1,8,128]{4,3,2,1,0:T(8,128)}), f32[128,1,1,8,128]{4,3,2,1,0:T(8,128)S(1)}, u32[]{:S(2)}, u32[]{:S(2)}) async-start(f32[128,1,1,8,128]{4,3,2,1,0:T(8,128)} %bitcast.14), calls=%async_computation.1 | async-start | bytes 1048576 | tf_op jit(solution)/shard_map/all_to_all | solution.py:27
  150.5 24.0 %all-to-all-start.2 = ((s32[128,1,1,8]{3,2,1,0:T(1,128)}), s32[128,1,1,8]{3,2,1,0:T(1,128)S(1)}, u32[]{:S(2)}, u32[]{:S(2)}) async-start(s32[128,1,1,8]{3,2,1,0:T(1,128)} %bitcast.21), calls=%async_computation.2 | async-start | bytes 131072 | tf_op jit(solution)/shard_map/all_to_all | solution.py:27
  167.5 30.0 %copy-start.25 = (pred[512]{0:T(512)(128)(4,1)S(1)}, pred[512]{0:T(512)(128)(4,1)}, u32[]{:S(2)}) copy-start(pred[512]{0:T(512)(128)(4,1)} %get-tuple-element.24) | copy-start | bytes 1540
  174.5 23.0 %all-to-all-start.3 = ((f32[128,1,1,8,128]{4,3,2,1,0:T(8,128)}), f32[128,1,1,8,128]{4,3,2,1,0:T(8,128)}, u32[]{:S(2)}, u32[]{:S(2)}) async-start(f32[128,1,1,8,128]{4,3,2,1,0:T(8,128)} %fusion.81), calls=%async_computation.3 | async-start | bytes 1048576 | tf_op jit(solution)/shard_map/all_to_all | solution.py:27
  185.1 49.3 %copy-start.22 = (s32[512]{0:T(512)}, s32[512]{0:T(512)S(1)}, u32[]{:S(2)}) copy-start(s32[512]{0:T(512)S(1)} %get-tuple-element.10) | copy-start | bytes 6148
  242.9 45.5 %copy-start.28 = (pred[512]{0:T(512)(128)(4,1)S(1)}, pred[512]{0:T(512)(128)(4,1)}, u32[]{:S(2)}) copy-start(pred[512]{0:T(512)(128)(4,1)} %get-tuple-element.28) | copy-start | bytes 1540
  292.1 29.6 %all-to-all-start.4 = ((f32[128,1,1,8,128]{4,3,2,1,0:T(8,128)}), f32[128,1,1,8,128]{4,3,2,1,0:T(8,128)}, u32[]{:S(2)}, u32[]{:S(2)}) async-start(f32[128,1,1,8,128]{4,3,2,1,0:T(8,128)} %bitcast.174), calls=%async_computation.4 | async-start | bytes 1048576 | tf_op jit(solution)/shard_map/all_to_all | solution.py:27
  297.9 47.9 %copy-start.17 = (pred[1024]{0:T(1024)(128)(4,1)}, pred[1024]{0:T(1024)(128)(4,1)S(1)}, u32[]{:S(2)}) copy-start(pred[1024]{0:T(1024)(128)(4,1)S(1)} %compare_and_fusion.5) | copy-start | bytes 3076
  321.7 25.8 %all-to-all-start.5 = ((s32[128,1,1,8]{3,2,1,0:T(1,128)}), s32[128,1,1,8]{3,2,1,0:T(1,128)S(1)}, u32[]{:S(2)}, u32[]{:S(2)}) async-start(s32[128,1,1,8]{3,2,1,0:T(1,128)} %bitcast.50), calls=%async_computation.5 | async-start | bytes 131072 | tf_op jit(solution)/shard_map/all_to_all | solution.py:27
  339.8 20.0 %copy-start.12 = (pred[512,16]{0,1:T(8,128)(4,1)S(1)}, pred[512,16]{0,1:T(8,128)(4,1)}, u32[]{:S(2)}) copy-start(pred[512,16]{0,1:T(8,128)(4,1)} %get-tuple-element.38) | copy-start | bytes 24580
  345.8 13.7 %copy-start.19 = (pred[1024]{0:T(1024)(128)(4,1)}, pred[1024]{0:T(1024)(128)(4,1)S(1)}, u32[]{:S(2)}) copy-start(pred[1024]{0:T(1024)(128)(4,1)S(1)} %get-tuple-element.23) | copy-start | bytes 3076
  347.4 12.1 %copy-start.8 = (s32[128,1,1,8]{3,2,1,0:T(1,128)}, s32[128,1,1,8]{3,2,1,0:T(1,128)S(1)}, u32[]{:S(2)}) copy-start(s32[128,1,1,8]{3,2,1,0:T(1,128)S(1)} %all-to-all-done.5) | copy-start | bytes 12292
  347.4 25.1 %all-to-all-start.6 = ((f32[128,1,1,8,128]{4,3,2,1,0:T(8,128)}), f32[128,1,1,8,128]{4,3,2,1,0:T(8,128)}, u32[]{:S(2)}, u32[]{:S(2)}) async-start(f32[128,1,1,8,128]{4,3,2,1,0:T(8,128)} %fusion.79), calls=%async_computation.6 | async-start | bytes 1048576 | tf_op jit(solution)/shard_map/all_to_all | solution.py:27
  380.2 29.3 %copy-start.10 = (pred[512,16]{1,0:T(8,128)(4,1)S(1)}, pred[512,16]{1,0:T(8,128)(4,1)}, u32[]{:S(2)}) copy-start(pred[512,16]{1,0:T(8,128)(4,1)} %copy.50) | copy-start | bytes 24580
  418.0 45.1 %copy-start.14 = (s32[1024]{0:T(1024)S(1)}, s32[1024]{0:T(1024)}, u32[]{:S(2)}) copy-start(s32[1024]{0:T(1024)} %copy-done.13) | copy-start | bytes 12292
  418.0 45.1 %copy-start.23 = (s32[512]{0:T(512)S(1)}, s32[512]{0:T(512)}, u32[]{:S(2)}) copy-start(s32[512]{0:T(512)} %copy-done.22) | copy-start | bytes 6148
  418.0 45.1 %copy-start.27 = (pred[512]{0:T(512)(128)(4,1)S(1)}, pred[512]{0:T(512)(128)(4,1)}, u32[]{:S(2)}) copy-start(pred[512]{0:T(512)(128)(4,1)} %get-tuple-element.20) | copy-start | bytes 1540
  418.0 55.1 %copy-start.18 = (pred[1024]{0:T(1024)(128)(4,1)S(1)}, pred[1024]{0:T(1024)(128)(4,1)}, u32[]{:S(2)}) copy-start(pred[1024]{0:T(1024)(128)(4,1)} %copy-done.17) | copy-start | bytes 3076
  418.0 55.1 %copy-start.20 = (pred[1024]{0:T(1024)(128)(4,1)S(1)}, pred[1024]{0:T(1024)(128)(4,1)}, u32[]{:S(2)}) copy-start(pred[1024]{0:T(1024)(128)(4,1)} %copy-done.19) | copy-start | bytes 3076
  463.2 18.1 %copy-start.16 = (f32[1024]{0:T(1024)S(1)}, f32[1024]{0:T(1024)}, u32[]{:S(2)}) copy-start(f32[1024]{0:T(1024)} %get-tuple-element.22) | copy-start | bytes 12292
  466.8 30.0 %all-to-all-start.7 = ((f32[128,1,1,8,128]{4,3,2,1,0:T(8,128)}), f32[128,1,1,8,128]{4,3,2,1,0:T(8,128)}, u32[]{:S(2)}, u32[]{:S(2)}) async-start(f32[128,1,1,8,128]{4,3,2,1,0:T(8,128)} %bitcast.175), calls=%async_computation.7 | async-start | bytes 1048576 | tf_op jit(solution)/shard_map/all_to_all | solution.py:27
  506.1 17.3 %copy-start.9 = (s32[128,1,1,8]{3,2,1,0:T(1,128)S(1)}, s32[128,1,1,8]{3,2,1,0:T(1,128)}, u32[]{:S(2)}) copy-start(s32[128,1,1,8]{3,2,1,0:T(1,128)} %copy-done.8) | copy-start | bytes 12292
  513.2 26.5 %all-to-all-start.8 = ((f32[128,1,1,8,128]{4,3,2,1,0:T(8,128)}), f32[128,1,1,8,128]{4,3,2,1,0:T(8,128)}, u32[]{:S(2)}, u32[]{:S(2)}) async-start(f32[128,1,1,8,128]{4,3,2,1,0:T(8,128)} %fusion.77), calls=%async_computation.8 | async-start | bytes 1048576 | tf_op jit(solution)/shard_map/all_to_all | solution.py:27
  526.2 13.5 %copy-start.3 = (f32[4096,128]{1,0:T(8,128)}, f32[4096,128]{1,0:T(8,128)S(1)}, u32[]{:S(2)}) copy-start(f32[4096,128]{1,0:T(8,128)S(1)} %scatter_custom_fusion.23) | copy-start | bytes 6291460
  535.1 12.4 %copy-start.1 = (s32[4096]{0:T(1024)S(1)}, s32[4096]{0:T(1024)}, u32[]{:S(2)}) copy-start(s32[4096]{0:T(1024)} %param.25) | copy-start | bytes 49156
  535.1 4.7 copy-start.24
  539.7 7.7 %copy-start.2 = (f32[8192]{0:T(1024)}, f32[8192]{0:T(1024)S(1)}, u32[]{:S(2)}) copy-start(f32[8192]{0:T(1024)S(1)} %scatter_fusion.5) | copy-start | bytes 98308
where the time goes:
time: 557 us; the launch traced here: 548 us
  other arithmetic  254 us (46%)
  local copies, waits for them, and re-layouts  193 us (35%)
  starting transfers between devices  83.4 us (15%)
  waiting for transfers between devices  16.2 us (3%)
    scatter-add x3, other arithmetic, body(): jax.ops.segment_sum(spread, picks.reshape(-1), num_segments=slots_dev)  136 us
    gather x3, local copies, waits for them, and re-layouts, body(): pooled = jnp.mean(jnp.take(cache_values, picks, axis=0), axis=1)  86.3 us
    all_to_all x9, starting transfers between devices, exchange_both(): lax.all_to_all(blocks, axis, split_axis=0, concat_axis=0, tiled=True)  83.4 us
    scatter-add x3, other arithmetic, body(): jax.ops.segment_sum(got_values, got_index, num_segments=rows_dev + 1)  26.6 us
    scatter x3, other arithmetic, body(): table = table.at[got_index].set(answer, mode='drop')  25 us
    scatter x3, other arithmetic, body(): cache_values = cache_values.at[listed].set(fresh)  23 us
    gather x3, local copies, waits for them, and re-layouts, body(): old_accum = jnp.take(accum, safe_index)  18.5 us
    all_to_all x9, waiting for transfers between devices, exchange_both(): lax.all_to_all(blocks, axis, split_axis=0, concat_axis=0, tiled=True)  16.2 us
  transfers between devices with their start and end apart: 9, of which 3 were waited for; matrix products, arithmetic and copies ran while one was open for 40% of the time, Pallas kernels for 0%

commit v1 on v0

v1 whole, which is shorter than its diff:
```python
import functools

import jax
import jax.numpy as jnp
from jax import lax
from jax.experimental import pallas as pl
from jax.experimental.pallas import tpu as pltpu
from jax.sharding import PartitionSpec as P

LEARN_RATE = 0.3
MESH = pl.DeviceIdType.MESH
F32, BF16, I32 = jnp.float32, jnp.bfloat16, jnp.int32

N = 128
CAP = 8
W = 128
SLOTS = 4096
BLOCK = 32
ROWS = 8192
BAGS = 512
BAG = 16
STEPS = 3
GROUPS = 4


def iota(shape, dim):
    return lax.broadcasted_iota(I32, shape, dim)


def one_hot(mask):
    return jnp.where(mask, 1.0, 0.0).astype(BF16)


def parts(x):
    hi = x.astype(BF16)
    return jnp.concatenate([hi, (x - hi.astype(F32)).astype(BF16)], axis=1)


def joined(y):
    return y[:, :W] + y[:, W:]


def dot(a, b):
    return jnp.dot(a, b, preferred_element_type=F32)


def dot_nt(a, b):
    return lax.dot_general(a, b, (((1,), (1,)), ((), ())), preferred_element_type=F32)


def dot_tn(a, b):
    return lax.dot_general(a, b, (((0,), (0,)), ((), ())), preferred_element_type=F32)


def exact_bf16(x):
    return x.astype(BF16)


def kernel(
    owner_sm, keys_ref, dirty_ref, rows_ref, accum_ref, table_hbm, cache_hbm, pending_hbm, targets_hbm,
    table_out, accum_out, cache_out, pending_out,
    table, cache, waiting, targets, counts, sel, mix, pick, base, flush, fresh, freshp, bag_grad,
    send_f, recv_f, send_b, recv_b, idx_send, idx_recv, idx_sm, inv_v, inv_sm,
    place, ycol, yrow, same, share, old, acc_old, delta,
    in_sem, sm_sem, out_sem, isend_sem, irecv_sem, fsend_sem, frecv_sem, bsend_sem, brecv_sem,
):
    gx, gy = lax.axis_index("gx"), lax.axis_index("gy")
    me = gx * 16 + gy

    def partner(k):
        p = lax.rem(me + k, N)
        return p, (p // 16, lax.rem(p, 16))

    loads = [
        pltpu.make_async_copy(cache_hbm, cache, in_sem.at[0]),
        pltpu.make_async_copy(targets_hbm, targets, in_sem.at[1]),
        pltpu.make_async_copy(pending_hbm, waiting, in_sem.at[2]),
        pltpu.make_async_copy(table_hbm, table, in_sem.at[3]),
    ]
    for load in loads:
        load.start()
    barrier = pltpu.get_barrier_semaphore()

    def greet(k, _):
        pl.semaphore_signal(barrier, inc=1, device_id=partner(k)[1], device_id_type=MESH)
        return 0

    lax.fori_loop(1, N, greet, 0)

    lane_i = iota((BLOCK, 256), 1)
    sub_i = iota((BLOCK, 256), 0)
    before = one_hot(sub_i < lane_i % BLOCK)
    spread = one_hot(sub_i == lane_i % BLOCK)
    rows = rows_ref[...]
    local = rows - (rows // ROWS) * ROWS
    local_hi = local // 128
    local_lo = local - local_hi * 128
    rep_hi = dot(exact_bf16(local_hi.astype(F32)), spread)
    rep_lo = dot(exact_bf16(local_lo.astype(F32)), spread)
    want = (iota((N, 256), 1) // BLOCK).astype(F32)
    inner = (iota((N, 256), 1) % BLOCK).astype(F32)
    found = jnp.zeros((N, W), F32)
    at_hi = jnp.zeros((N, W), F32)
    at_lo = jnp.zeros((N, W), F32)
    at_in = jnp.zeros((N, W), F32)
    for t in range(STEPS):
        d = dirty_ref[t : t + 1, :]
        blk = d // BLOCK
        hot_b = one_hot(iota((N, BAGS), 0) == blk)
        hot_i = one_hot(iota((BLOCK, BAGS), 0) == d - blk * BLOCK)
        listed = exact_bf16(dot_nt(hot_b, hot_i))
        rank = dot(listed, before)
        there = dot(listed, spread)
        chosen = jnp.where((rank == want) & (there > 0.5), 1.0, 0.0)
        gather = one_hot(iota((256, W), 0) // BLOCK + t * CAP == iota((256, W), 1))
        found = found + dot(exact_bf16(chosen), gather)
        at_hi = at_hi + dot(exact_bf16(chosen * rep_hi), gather)
        at_lo = at_lo + dot(exact_bf16(chosen * rep_lo), gather)
        at_in = at_in + dot(exact_bf16(chosen * inner), gather)
    owner_col = rows[:, :1] // ROWS
    perm = one_hot(owner_col == iota((N, N), 1))
    sent_found = dot_tn(perm, exact_bf16(found))
    sent_hi = dot_tn(perm, exact_bf16(at_hi))
    sent_lo = dot_tn(perm, exact_bf16(at_lo))
    sent = jnp.where(sent_found > 0.5, sent_hi * 128.0 + sent_lo, -1.0).astype(I32)
    idx_send[...] = sent.reshape(N, 1, W)
    block_row = exact_bf16(iota((8, N), 1).astype(F32))
    inv_v[...] = jnp.minimum(dot(block_row, perm), N - 1.0).astype(I32)
    inv_copy = pltpu.make_async_copy(inv_v, inv_sm, sm_sem.at[0])
    inv_copy.start()
    in_block = jnp.where(found > 0.5, at_in, -1.0)
    for t in range(STEPS):
        rep8 = one_hot(iota((W, 256), 0) == iota((W, 256), 1) % CAP + t * CAP)
        wide_in = dot(exact_bf16(in_block), rep8)
        for g in range(GROUPS):
            jj = iota((N, 256), 0) - g * 32
            here = jj == iota((N, 256), 1) // CAP
            part = exact_bf16(jnp.where(here, wide_in, 0.0))
            inside = dot(jnp.ones((8, N), BF16), part)
            offset = (iota((8, 256), 1) // CAP * BLOCK).astype(F32)
            place[t, g] = jnp.where(inside < -0.5, -1.0, inside + offset).astype(I32)

    def build_counts(t):
        def group(g, _):
            slot = keys_ref[t, pl.ds(g, 1), :]
            head = slot // 128
            key = head * 16 + iota((1, 256), 1) // BAG
            a = one_hot(iota((512, 256), 0) == key)
            b = one_hot(iota((128, 256), 0) == slot - head * 128)
            r = dot_nt(a, b).astype(BF16)
            row = pl.multiple_of(g * 16, 16)
            for h in range(32):
                counts[h // 8, pl.ds(row, 16), (h % 8) * 128 : (h % 8 + 1) * 128] = r[h * 16 : (h + 1) * 16]
            return 0

        lax.fori_loop(0, 32, group, 0)

    def build_sel(t):
        def group(g, _):
            sel[t, g] = one_hot(iota((1024, 256), 0) == place[t, g, :1, :])
            return 0

        lax.fori_loop(0, GROUPS, group, 0)

    def build_flush_plan(t):
        def group(g, _):
            s = sel[t, g]
            mix[g] = dot(counts[g], s).T.astype(BF16)
            base[g] = joined(dot_tn(s, parts(waiting[pl.ds(pl.multiple_of(g * 1024, 1024), 1024), :])))
            return 0

        lax.fori_loop(0, GROUPS, group, 0)

    def pooled_base(masked_by):
        total = jnp.zeros((BAGS, 2 * W), F32)
        for g in range(GROUPS):
            c = cache[g * 1024 : (g + 1) * 1024, :]
            if masked_by is not None:
                gone = dot(sel[masked_by, g], jnp.ones((256, W), BF16))
                c = jnp.where(gone > 0.5, 0.0, c)
            total = total + dot(counts[g], parts(c))
        return joined(total)

    def build_pick(t_prev):
        def group(g, _):
            pick[g] = dot(counts[g], sel[t_prev, g]).astype(BF16)
            return 0

        lax.fori_loop(0, GROUPS, group, 0)

    def update_waiting(t):
        def group(g, _):
            at = pl.ds(pl.multiple_of(g * 1024, 1024), 1024)
            w = waiting[at, :] + joined(dot_tn(counts[g], bag_grad[...]))
            gone = dot(sel[t, g], jnp.ones((256, W), BF16))
            waiting[at, :] = jnp.where(gone > 0.5, 0.0, w)
            return 0

        lax.fori_loop(0, GROUPS, group, 0)

    def update_cache(t):
        def group(g, _):
            at = pl.ds(pl.multiple_of(g * 1024, 1024), 1024)
            s = sel[t, g]
            new = joined(dot(s, freshp[g]))
            gone = dot(s, jnp.ones((256, W), BF16))
            cache[at, :] = jnp.where(gone > 0.5, new, cache[at, :])
            return 0

        lax.fori_loop(0, GROUPS, group, 0)

    def exchange_start(src, dst, send_sem, recv_sem):
        def one(k, _):
            p, target = partner(k)
            pltpu.make_async_remote_copy(
                src_ref=src.at[p], dst_ref=dst.at[me], send_sem=send_sem, recv_sem=recv_sem,
                device_id=target, device_id_type=MESH,
            ).start()
            return 0

        lax.fori_loop(1, N, one, 0)
        dst[me] = src[me]

    def exchange_wait(src, dst, send_sem, recv_sem):
        all_of = pltpu.make_async_remote_copy(
            src_ref=src.at[pl.ds(0, N - 1)], dst_ref=dst.at[pl.ds(0, N - 1)], send_sem=send_sem,
            recv_sem=recv_sem, device_id=partner(1)[1], device_id_type=MESH,
        )
        all_of.wait_send()
        all_of.wait_recv()

    def owner_plan(t):
        x = jnp.broadcast_to(idx_recv[...], (N, CAP, W)).reshape(N * CAP, W)
        e = iota((N * CAP, W), 0)
        mine = iota((N * CAP, W), 1) == t * CAP + e % CAP
        col = jnp.sum(jnp.where(mine, x, 0).astype(F32), axis=1, keepdims=True)
        wide = jnp.broadcast_to(col, (N * CAP, W))
        ycol[...] = wide.astype(I32)
        for b in range(8):
            turned = wide[b * 128 : (b + 1) * 128, :].T
            yrow[:, b * 128 : (b + 1) * 128] = turned[:8, :].astype(I32)
        y = yrow[:1, :]

        def chunk(c, _):
            at = pl.ds(pl.multiple_of(c * 256, 256), 256)
            m = one_hot(ycol[at, :1] == y)
            same[at, :] = m
            share[at, :] = 1.0 / dot(m, jnp.ones((1024, W), BF16))
            return 0

        lax.fori_loop(0, 4, chunk, 0)
        yc = ycol[...]
        head = yc // 128
        hot = one_hot(iota((N * CAP, W), 1) == head)[:, :64]
        a = accum_out[...]
        a1 = a.astype(BF16)
        a2 = (a - a1.astype(F32)).astype(BF16)
        a3 = (a - a1.astype(F32) - a2.astype(F32)).astype(BF16)
        got = dot(hot, a1) + dot(hot, a2) + dot(hot, a3)
        got = jnp.where(iota((N * CAP, W), 1) == yc - head * 128, got, 0.0)
        acc = jnp.sum(got, axis=1, keepdims=True)
        acc_old[...] = jnp.broadcast_to(jnp.where(yc[:, :1] < 0, 1.0, acc), (N * CAP, W))

        def fetch(src, _):
            for k in range(CAP):
                i = jnp.clip(idx_sm[src, 0, t * CAP + k], 0, ROWS - 1)
                old[src, k : k + 1, :] = table[pl.ds(i, 1), :]
            return 0

        lax.fori_loop(0, N, fetch, 0)

    def owner_update(t):
        got = parts(recv_f[t].reshape(N * CAP, W))
        total = joined(dot(same[...], got))
        extra = jnp.mean(total * total, axis=1, keepdims=True)
        acc = acc_old[...] + extra
        step = LEARN_RATE * total / jnp.sqrt(acc)
        send_b[t] = (old[...].reshape(N * CAP, W) - step).reshape(N, CAP, W)
        delta[:, :W] = step * share[...]
        delta[:, W:] = extra * share[...]

    def owner_store(t):
        y = yrow[:1, :]
        step = parts(delta[:, :W])

        def chunk(c, _):
            at = pl.ds(pl.multiple_of(c * 1024, 1024), 1024)
            hot = one_hot(iota((1024, 1024), 0) + c * 1024 == y)
            table[at, :] = table[at, :] - joined(dot(hot, step))
            return 0

        lax.fori_loop(0, ROWS // 1024, chunk, 0)
        yc = ycol[...]
        head = yc // 128
        tail = jnp.where(iota((N * CAP, W), 1) == yc - head * 128, delta[:, W:], 0.0)
        hot = one_hot(iota((64, N * CAP), 0) == y // 128)
        accum_out[...] = accum_out[...] + joined(dot(hot, parts(tail)))

    accum_out[...] = accum_ref[...]
    build_counts(0)
    pl.semaphore_wait(barrier, N - 1)
    exchange_start(idx_send, idx_recv, isend_sem.at[0], irecv_sem.at[0])
    build_sel(0)
    loads[0].wait()
    pooled = pooled_base(None)
    loads[2].wait()
    build_flush_plan(0)
    loads[1].wait()
    inv_copy.wait()
    for t in range(STEPS):
        if t > 0:
            pooled = base_pooled
            for g in range(GROUPS):
                pooled = pooled + joined(dot(pick[g], freshp[g]))
        grad = (pooled * (1.0 / BAG) - targets[t]) * (1.0 / BAG)
        bag_grad[...] = parts(grad)
        for g in range(GROUPS):
            out = base[g] + joined(dot(mix[g], bag_grad[...]))
            flush[g * 32 : (g + 1) * 32] = out.reshape(32, CAP, W)

        def to_owner(o, _):
            send_f[t, o] = flush[jnp.clip(inv_sm[0, o], 0, N - 1)]
            return 0

        lax.fori_loop(0, N, to_owner, 0, unroll=8)
        exchange_start(send_f.at[t], recv_f.at[t], fsend_sem.at[t], frecv_sem.at[t])
        update_waiting(t)
        if t == STEPS - 1:
            pending_store = pltpu.make_async_copy(waiting, pending_out, out_sem.at[0])
            pending_store.start()
        if t == 0:
            exchange_wait(idx_send, idx_recv, isend_sem.at[0], irecv_sem.at[0])
            idx_copy = pltpu.make_async_copy(idx_recv, idx_sm, sm_sem.at[1])
            idx_copy.start()
            loads[3].wait()
            idx_copy.wait()
        owner_plan(t)
        if t > 0:
            update_cache(t - 1)
        if t < STEPS - 1:
            build_counts(t + 1)
        exchange_wait(send_f.at[t], recv_f.at[t], fsend_sem.at[t], frecv_sem.at[t])
        owner_update(t)
        exchange_start(send_b.at[t], recv_b.at[t], bsend_sem.at[t], brecv_sem.at[t])
        if t < STEPS - 1:
            build_sel(t + 1)
            build_pick(t)
            base_pooled = pooled_base(t)
            build_flush_plan(t + 1)
        owner_store(t)
        if t == STEPS - 1:
            table_store = pltpu.make_async_copy(table, table_out, out_sem.at[1])
            table_store.start()
        exchange_wait(send_b.at[t], recv_b.at[t], bsend_sem.at[t], brecv_sem.at[t])

        def from_owner(j, _):
            fresh[j] = recv_b[t, jnp.clip(owner_sm[j], 0, N - 1)]
            return 0

        lax.fori_loop(0, N, from_owner, 0, unroll=8)
        for g in range(GROUPS):
            freshp[g] = parts(fresh[g * 32 : (g + 1) * 32].reshape(256, W))
    update_cache(STEPS - 1)
    cache_store = pltpu.make_async_copy(cache, cache_out, out_sem.at[2])
    cache_store.start()
    pending_store.wait()
    table_store.wait()
    cache_store.wait()


def body(table, accum, cache_values, cache_rows, pending, batch_slots, targets, dirty):
    keys = batch_slots.reshape(STEPS, 32, 256)
    rows = cache_rows.reshape(N, BLOCK)
    owners = rows[:, 0] // ROWS
    vmem = pl.BlockSpec(memory_space=pltpu.VMEM)
    smem = pl.BlockSpec(memory_space=pltpu.SMEM)
    hbm = pl.BlockSpec(memory_space=pl.ANY)
    dma = pltpu.SemaphoreType.DMA
    tiles = (N, CAP, W)
    new_table, new_accum, new_cache, new_pending = pl.pallas_call(
        kernel,
        out_shape=(
            jax.ShapeDtypeStruct((ROWS, W), F32),
            jax.ShapeDtypeStruct((64, W), F32),
            jax.ShapeDtypeStruct((SLOTS, W), F32),
            jax.ShapeDtypeStruct((SLOTS, W), F32),
        ),
        in_specs=[smem, vmem, vmem, vmem, vmem, hbm, hbm, hbm, hbm],
        out_specs=(hbm, vmem, hbm, hbm),
        scratch_shapes=[
            pltpu.VMEM((ROWS, W), F32),
            pltpu.VMEM((SLOTS, W), F32),
            pltpu.VMEM((SLOTS, W), F32),
            pltpu.VMEM((STEPS, BAGS, W), F32),
            pltpu.VMEM((GROUPS, BAGS, 1024), BF16),
            pltpu.VMEM((STEPS, GROUPS, 1024, 256), BF16),
            pltpu.VMEM((GROUPS, 256, BAGS), BF16),
            pltpu.VMEM((GROUPS, BAGS, 256), BF16),
            pltpu.VMEM((GROUPS, 256, W), F32),
            pltpu.VMEM(tiles, F32),
            pltpu.VMEM(tiles, F32),
            pltpu.VMEM((GROUPS, 256, 2 * W), BF16),
            pltpu.VMEM((BAGS, 2 * W), BF16),
            pltpu.VMEM((STEPS, *tiles), F32),
            pltpu.VMEM((STEPS, *tiles), F32),
            pltpu.VMEM((STEPS, *tiles), F32),
            pltpu.VMEM((STEPS, *tiles), F32),
            pltpu.VMEM((N, 1, W), I32),
            pltpu.VMEM((N, 1, W), I32),
            pltpu.SMEM((N, 1, W), I32),
            pltpu.VMEM((8, N), I32),
            pltpu.SMEM((8, N), I32),
            pltpu.VMEM((STEPS, GROUPS, 8, 256), I32),
            pltpu.VMEM((N * CAP, W), I32),
            pltpu.VMEM((8, N * CAP), I32),
            pltpu.VMEM((N * CAP, N * CAP), BF16),
            pltpu.VMEM((N * CAP, W), F32),
            pltpu.VMEM(tiles, F32),
            pltpu.VMEM((N * CAP, W), F32),
            pltpu.VMEM((N * CAP, 2 * W), F32),
            dma((4,)),
            dma((2,)),
            dma((3,)),
            dma((1,)),
            dma((1,)),
            dma((STEPS,)),
            dma((STEPS,)),
            dma((STEPS,)),
            dma((STEPS,)),
        ],
        compiler_params=pltpu.CompilerParams(
            collective_id=0, has_side_effects=True, vmem_limit_bytes=56 * 1024 * 1024
        ),
    )(
        owners, keys, dirty, rows, accum.reshape(64, W), table, cache_values, pending, targets
    )
    return new_table, new_accum.reshape(-1), new_cache, new_pending


def solution(mesh):
    in_specs = (
        P(("gx", "gy"), None),
        P(("gx", "gy")),
        P(("gx", "gy"), None),
        P(("gx", "gy")),
        P(("gx", "gy"), None),
        P(None, ("gx", "gy"), None),
        P(None, ("gx", "gy"), None),
        P(None, ("gx", "gy")),
    )
    out_specs = (
        P(("gx", "gy"), None),
        P(("gx", "gy")),
        P(("gx", "gy"), None),
        P(("gx", "gy"), None),
    )
    return jax.shard_map(body, mesh=mesh, in_specs=in_specs, out_specs=out_specs, check_vma=False)
```

time: 557 us -> 145 us (0.26); the launches traced: 548 us -> 145 us
  other arithmetic: 254 us -> 0.53 us
  local copies, waits for them, and re-layouts: 193 us -> 11.9 us
  Pallas kernels: 0 us -> 132 us
  starting transfers between devices: 83.4 us -> 0 us
  waiting for transfers between devices: 16.2 us -> 0 us
    scatter-add x6 -> x0, other arithmetic: 162 us -> none  [the longest x3 136 us: body(): jax.ops.segment_sum(spread, picks.reshape(-1), num_segments=slots_dev)]
    gather x15 -> x0, local copies, waits for them, and re-layouts: 144 us -> none  [the longest x3 86.3 us: body(): pooled = jnp.mean(jnp.take(cache_values, picks, axis=0), axis=1)]
    pallas_call x0 -> x1, Pallas kernels: none -> 132 us  [body(): pl.pallas_call(kernel, out_shape=(jax.ShapeDtypeStruct((ROWS, W), F32), j...]
    all_to_all x9 -> x0, starting transfers between devices: 83.4 us -> none  [exchange_both(): lax.all_to_all(blocks, axis, split_axis=0, concat_axis=0, tiled=True)]
    scatter x9 -> x0, other arithmetic: 58.9 us -> none  [the longest x3 25 us: body(): table = table.at[got_index].set(answer, mode='drop')]
    scatter x9 -> x0, local copies, waits for them, and re-layouts: 28.6 us -> none  [the longest x3 13.3 us: body(): accum = accum.at[got_index].set(fresh_accum, mode='drop')]
    reduce_sum x9 -> x0, other arithmetic: 17.9 us -> none  [the longest x3 16 us: body(): pooled = jnp.mean(jnp.take(cache_values, picks, axis=0), axis=1)]
    all_to_all x9 -> x0, waiting for transfers between devices: 16.2 us -> none  [exchange_both(): lax.all_to_all(blocks, axis, split_axis=0, concat_axis=0, tiled=True)]
  transfers between devices with their start and end apart: 9 -> 0, of which waited for: 3 -> 0; matrix products, arithmetic and copies ran while one was open for 40% -> 0% of each run, Pallas kernels for 0% -> 0%
where the time goes in v1:
time: 145 us
  Pallas kernels  132 us (91%)
  local copies, waits for them, and re-layouts  11.9 us (8%)
    pallas_call x1, Pallas kernels, body(): pl.pallas_call(kernel, out_shape=(jax.ShapeDtypeStruct((ROWS, W), F32), j...  132 us
    unnamed x13, local copies, waits for them, and re-layouts  10.1 us

profile of v1, /device:TPU:1, one launch (start us, length us, event | category | flops | bytes accessed | tf_op | source)
XLA Modules:
  0.0 144.9 jit_solution(2159973304930807902)
XLA Ops:
  0.6 0.8 reshape.20.rows_ref
  1.4 0.0 copy-start.2
  1.4 0.1 slice_reduce_fusion
  1.5 0.5 and_select_fusion.owner_sm
  2.1 1.2 copy.13
  3.2 1.0 reshape.21.keys_ref
  4.2 0.0 copy-done.2
  4.2 131.7 %shard_map.111 = (f32[8192,128]{1,0:T(8,128)}, f32[64,128]{1,0:T(8,128)}, f32[4096,128]{1,0:T(8,128)}, f32[4096,128]{1,0:T(8,128)}) custom-call(s32[128]{0:T(128)} %and_select_fusion.owner_sm, s32[3,32,256]{2,1,0:T(8,128)} %reshape.21.keys_ref, s32[3,512]{1,0:T(4,128)} %dirty_ref.1, s32[128,32]{1,0:T(8,128)} %copy-done.2, f32[64,128]{1,0:T(8,128)} %bitcast.2, ...), custom_call_target="tpu_custom_call" | custom-call | tf_op jit(solution)/shard_map/pallas_call | solution.py:380
  135.9 0.0 copy-start.3
  135.9 0.0 copy-start.1
  136.0 4.6 %copy.18 = f32[8192,128]{1,0:T(8,128)} copy(f32[8192,128]{1,0:T(8,128)} %get-tuple-element.16) | data formatting | bytes 8388608
  140.6 0.0 copy-done.3
  140.6 0.6 copy.19
  141.2 0.0 copy-done.1
  141.2 0.0 copy-start
  141.2 1.3 copy.20
  142.5 1.0 copy-done
  143.5 1.3 copy.21
Async XLA Ops:
  1.4 2.8 %copy-start.2 = (s32[128,32]{1,0:T(8,128)}, s32[128,32]{1,0:T(8,128)S(1)}, u32[]{:S(2)}) copy-start(s32[128,32]{1,0:T(8,128)S(1)} %reshape.20.rows_ref) | copy-start | bytes 49156
  135.9 4.6 %copy-start.3 = (f32[64,128]{1,0:T(8,128)S(1)}, f32[64,128]{1,0:T(8,128)}, u32[]{:S(2)}) copy-start(f32[64,128]{1,0:T(8,128)} %get-tuple-element.9) | copy-start | bytes 98308
  135.9 5.3 %copy-start.1 = (f32[4096,128]{1,0:T(8,128)S(1)}, f32[4096,128]{1,0:T(8,128)}, u32[]{:S(2)}) copy-start(f32[4096,128]{1,0:T(8,128)} %get-tuple-element.18) | copy-start | bytes 6291460
  141.2 2.3 %copy-start = (f32[4096,128]{1,0:T(8,128)S(1)}, f32[4096,128]{1,0:T(8,128)}, u32[]{:S(2)}) copy-start(f32[4096,128]{1,0:T(8,128)} %get-tuple-element.19) | copy-start | bytes 6291460

commit v2 on v1

--- a/solution.py
+++ b/solution.py
@@ -8,7 +8,7 @@
 from jax.sharding import PartitionSpec as P
 
 LEARN_RATE = 0.3
-MESH = pl.DeviceIdType.MESH
+LOGICAL = pl.DeviceIdType.LOGICAL
 F32, BF16, I32 = jnp.float32, jnp.bfloat16, jnp.int32
 
 N = 128
@@ -58,18 +58,19 @@
 
 def kernel(
     owner_sm, keys_ref, dirty_ref, rows_ref, accum_ref, table_hbm, cache_hbm, pending_hbm, targets_hbm,
-    table_out, accum_out, cache_out, pending_out,
+    answers_out, idx_out, accum_out, cache_out, pending_out,
     table, cache, waiting, targets, counts, sel, mix, pick, base, flush, fresh, freshp, bag_grad,
     send_f, recv_f, send_b, recv_b, idx_send, idx_recv, idx_sm, inv_v, inv_sm,
-    place, ycol, yrow, same, share, old, acc_old, delta,
+    place, ycol, yrow, same, share, old, acc_old, gone, gotp, deltap, more,
     in_sem, sm_sem, out_sem, isend_sem, irecv_sem, fsend_sem, frecv_sem, bsend_sem, brecv_sem,
 ):
     gx, gy = lax.axis_index("gx"), lax.axis_index("gy")
     me = gx * 16 + gy
 
-    def partner(k):
-        p = lax.rem(me + k, N)
-        return p, (p // 16, lax.rem(p, 16))
+    quarter, inner_id = me // 32, lax.rem(me, 32)
+
+    def partner(q, k):
+        return lax.rem(quarter + q, 4) * 32 + lax.rem(inner_id + k, 32)
 
     loads = [
         pltpu.make_async_copy(cache_hbm, cache, in_sem.at[0]),
@@ -81,11 +82,13 @@
         load.start()
     barrier = pltpu.get_barrier_semaphore()
 
-    def greet(k, _):
-        pl.semaphore_signal(barrier, inc=1, device_id=partner(k)[1], device_id_type=MESH)
-        return 0
-
-    lax.fori_loop(1, N, greet, 0)
+    for q in range(4):
+
+        def greet(k, _):
+            pl.semaphore_signal(barrier, inc=1, device_id=partner(q, k), device_id_type=LOGICAL)
+            return 0
+
+        lax.fori_loop(0 if q else 1, 32, greet, 0)
 
     lane_i = iota((BLOCK, 256), 1)
     sub_i = iota((BLOCK, 256), 0)
@@ -153,11 +156,13 @@
                 counts[h // 8, pl.ds(row, 16), (h % 8) * 128 : (h % 8 + 1) * 128] = r[h * 16 : (h + 1) * 16]
             return 0
 
-        lax.fori_loop(0, 32, group, 0)
+        lax.fori_loop(0, 32, group, 0, unroll=4)
 
     def build_sel(t):
         def group(g, _):
-            sel[t, g] = one_hot(iota((1024, 256), 0) == place[t, g, :1, :])
+            s = one_hot(iota((1024, 256), 0) == place[t, g, :1, :])
+            sel[t, g] = s
+            gone[t, g] = dot(s, jnp.ones((256, W), BF16))
             return 0
 
         lax.fori_loop(0, GROUPS, group, 0)
@@ -165,7 +170,7 @@
     def build_flush_plan(t):
         def group(g, _):
             s = sel[t, g]
-            mix[g] = dot(counts[g], s).T.astype(BF16)
+            mix[g] = dot(counts[g], s).astype(BF16).T
             base[g] = joined(dot_tn(s, parts(waiting[pl.ds(pl.multiple_of(g * 1024, 1024), 1024), :])))
             return 0
 
@@ -176,8 +181,7 @@
         for g in range(GROUPS):
             c = cache[g * 1024 : (g + 1) * 1024, :]
             if masked_by is not None:
-                gone = dot(sel[masked_by, g], jnp.ones((256, W), BF16))
-                c = jnp.where(gone > 0.5, 0.0, c)
+                c = jnp.where(gone[masked_by, g] > 0.5, 0.0, c)
             total = total + dot(counts[g], parts(c))
         return joined(total)
 
@@ -192,8 +196,7 @@
         def group(g, _):
             at = pl.ds(pl.multiple_of(g * 1024, 1024), 1024)
             w = waiting[at, :] + joined(dot_tn(counts[g], bag_grad[...]))
-            gone = dot(sel[t, g], jnp.ones((256, W), BF16))
-            waiting[at, :] = jnp.where(gone > 0.5, 0.0, w)
+            waiting[at, :] = jnp.where(gone[t, g] > 0.5, 0.0, w)
             return 0
 
         lax.fori_loop(0, GROUPS, group, 0)
@@ -201,62 +204,62 @@
     def update_cache(t):
         def group(g, _):
             at = pl.ds(pl.multiple_of(g * 1024, 1024), 1024)
-            s = sel[t, g]
-            new = joined(dot(s, freshp[g]))
-            gone = dot(s, jnp.ones((256, W), BF16))
-            cache[at, :] = jnp.where(gone > 0.5, new, cache[at, :])
+            new = joined(dot(sel[t, g], freshp[g]))
+            cache[at, :] = jnp.where(gone[t, g] > 0.5, new, cache[at, :])
             return 0
 
         lax.fori_loop(0, GROUPS, group, 0)
 
-    def exchange_start(src, dst, send_sem, recv_sem):
+    def send_quarter(q, src, dst, send_sem, recv_sem):
         def one(k, _):
-            p, target = partner(k)
+            p = partner(q, k)
             pltpu.make_async_remote_copy(
                 src_ref=src.at[p], dst_ref=dst.at[me], send_sem=send_sem, recv_sem=recv_sem,
-                device_id=target, device_id_type=MESH,
+                device_id=p, device_id_type=LOGICAL,
             ).start()
             return 0
 
-        lax.fori_loop(1, N, one, 0)
+        lax.fori_loop(0 if q else 1, 32, one, 0)
+
+    def exchange_start(src, dst, send_sem, recv_sem):
+        for q in range(4):
+            send_quarter(q, src, dst, send_sem, recv_sem)
         dst[me] = src[me]
 
     def exchange_wait(src, dst, send_sem, recv_sem):
         all_of = pltpu.make_async_remote_copy(
             src_ref=src.at[pl.ds(0, N - 1)], dst_ref=dst.at[pl.ds(0, N - 1)], send_sem=send_sem,
-            recv_sem=recv_sem, device_id=partner(1)[1], device_id_type=MESH,
+            recv_sem=recv_sem, device_id=partner(0, 1), device_id_type=LOGICAL,
         )
         all_of.wait_send()
         all_of.wait_recv()
 
-    def owner_plan(t):
+    def plan_rows(t):
         x = jnp.broadcast_to(idx_recv[...], (N, CAP, W)).reshape(N * CAP, W)
         e = iota((N * CAP, W), 0)
         mine = iota((N * CAP, W), 1) == t * CAP + e % CAP
         col = jnp.sum(jnp.where(mine, x, 0).astype(F32), axis=1, keepdims=True)
         wide = jnp.broadcast_to(col, (N * CAP, W))
-        ycol[...] = wide.astype(I32)
+        ycol[t] = wide.astype(I32)
         for b in range(8):
             turned = wide[b * 128 : (b + 1) * 128, :].T
-            yrow[:, b * 128 : (b + 1) * 128] = turned[:8, :].astype(I32)
-        y = yrow[:1, :]
+            yrow[t, :, b * 128 : (b + 1) * 128] = turned[:8, :].astype(I32)
+        y = yrow[t, :1, :]
 
         def chunk(c, _):
             at = pl.ds(pl.multiple_of(c * 256, 256), 256)
-            m = one_hot(ycol[at, :1] == y)
+            m = one_hot(ycol[t, at, :1] == y)
             same[at, :] = m
             share[at, :] = 1.0 / dot(m, jnp.ones((1024, W), BF16))
             return 0
 
         lax.fori_loop(0, 4, chunk, 0)
-        yc = ycol[...]
+
+    def plan_values(t):
+        yc = ycol[t]
         head = yc // 128
         hot = one_hot(iota((N * CAP, W), 1) == head)[:, :64]
-        a = accum_out[...]
-        a1 = a.astype(BF16)
-        a2 = (a - a1.astype(F32)).astype(BF16)
-        a3 = (a - a1.astype(F32) - a2.astype(F32)).astype(BF16)
-        got = dot(hot, a1) + dot(hot, a2) + dot(hot, a3)
+        got = joined(dot(hot, parts(accum_out[...])))
         got = jnp.where(iota((N * CAP, W), 1) == yc - head * 128, got, 0.0)
         acc = jnp.sum(got, axis=1, keepdims=True)
         acc_old[...] = jnp.broadcast_to(jnp.where(yc[:, :1] < 0, 1.0, acc), (N * CAP, W))
@@ -264,39 +267,46 @@
         def fetch(src, _):
             for k in range(CAP):
                 i = jnp.clip(idx_sm[src, 0, t * CAP + k], 0, ROWS - 1)
-                old[src, k : k + 1, :] = table[pl.ds(i, 1), :]
+                old[pl.ds(src * CAP + k, 1), :] = table[pl.ds(i, 1), :]
             return 0
 
         lax.fori_loop(0, N, fetch, 0)
+        if t > 0:
+
+            def correct(c, _):
+                at = pl.ds(pl.multiple_of(c * 256, 256), 256)
+                moved = jnp.zeros((256, 2 * W), F32)
+                for s in range(t):
+                    m = one_hot(ycol[t, at, :1] == yrow[s, :1, :])
+                    moved = moved + dot(m, deltap[s])
+                old[at, :] = old[at, :] - joined(moved)
+                return 0
+
+            lax.fori_loop(0, 4, correct, 0)
 
     def owner_update(t):
-        got = parts(recv_f[t].reshape(N * CAP, W))
-        total = joined(dot(same[...], got))
-        extra = jnp.mean(total * total, axis=1, keepdims=True)
-        acc = acc_old[...] + extra
-        step = LEARN_RATE * total / jnp.sqrt(acc)
-        send_b[t] = (old[...].reshape(N * CAP, W) - step).reshape(N, CAP, W)
-        delta[:, :W] = step * share[...]
-        delta[:, W:] = extra * share[...]
-
-    def owner_store(t):
-        y = yrow[:1, :]
-        step = parts(delta[:, :W])
-
-        def chunk(c, _):
-            at = pl.ds(pl.multiple_of(c * 1024, 1024), 1024)
-            hot = one_hot(iota((1024, 1024), 0) + c * 1024 == y)
-            table[at, :] = table[at, :] - joined(dot(hot, step))
-            return 0
-
-        lax.fori_loop(0, ROWS // 1024, chunk, 0)
-        yc = ycol[...]
-        head = yc // 128
-        tail = jnp.where(iota((N * CAP, W), 1) == yc - head * 128, delta[:, W:], 0.0)
+        gotp[...] = parts(recv_f[t].reshape(N * CAP, W))
+        for q in range(4):
+            base_src = lax.rem(quarter + q, 4) * 32
+            at = pl.ds(pl.multiple_of(base_src * CAP, 256), 256)
+            total = joined(dot(same[at, :], gotp[...]))
+            extra = jnp.mean(total * total, axis=1, keepdims=True)
+            step = total * (LEARN_RATE * lax.rsqrt(acc_old[at, :] + extra))
+            send_b[t, pl.ds(base_src, 32)] = (old[at, :] - step).reshape(32, CAP, W)
+            deltap[t, at, :] = parts(step * share[at, :])
+            more[at, :] = extra * share[at, :]
+            send_quarter(q, send_b.at[t], recv_b.at[t], bsend_sem.at[t], brecv_sem.at[t])
+        recv_b[t, me] = send_b[t, me]
+
+    def accum_update(t):
+        y = yrow[t, :1, :]
+        yc = ycol[t]
+        tail = jnp.where(iota((N * CAP, W), 1) == yc - yc // 128 * 128, more[...], 0.0)
         hot = one_hot(iota((64, N * CAP), 0) == y // 128)
         accum_out[...] = accum_out[...] + joined(dot(hot, parts(tail)))
 
     accum_out[...] = accum_ref[...]
+    stores = []
     build_counts(0)
     pl.semaphore_wait(barrier, N - 1)
     exchange_start(idx_send, idx_recv, isend_sem.at[0], irecv_sem.at[0])
@@ -328,29 +338,35 @@
         if t == STEPS - 1:
             pending_store = pltpu.make_async_copy(waiting, pending_out, out_sem.at[0])
             pending_store.start()
+            stores.append(pending_store)
         if t == 0:
             exchange_wait(idx_send, idx_recv, isend_sem.at[0], irecv_sem.at[0])
             idx_copy = pltpu.make_async_copy(idx_recv, idx_sm, sm_sem.at[1])
             idx_copy.start()
+            plan_rows(0)
             loads[3].wait()
             idx_copy.wait()
-        owner_plan(t)
+        plan_values(t)
         if t > 0:
             update_cache(t - 1)
         if t < STEPS - 1:
             build_counts(t + 1)
         exchange_wait(send_f.at[t], recv_f.at[t], fsend_sem.at[t], frecv_sem.at[t])
         owner_update(t)
-        exchange_start(send_b.at[t], recv_b.at[t], bsend_sem.at[t], brecv_sem.at[t])
         if t < STEPS - 1:
             build_sel(t + 1)
             build_pick(t)
             base_pooled = pooled_base(t)
             build_flush_plan(t + 1)
-        owner_store(t)
-        if t == STEPS - 1:
-            table_store = pltpu.make_async_copy(table, table_out, out_sem.at[1])
-            table_store.start()
+            plan_rows(t + 1)
+        accum_update(t)
+        answers = pltpu.make_async_copy(send_b.at[t], answers_out.at[t], out_sem.at[2 + t])
+        answers.start()
+        stores.append(answers)
+        if t == 0:
+            idx_store = pltpu.make_async_copy(idx_recv, idx_out, out_sem.at[1])
+            idx_store.start()
+            stores.append(idx_store)
         exchange_wait(send_b.at[t], recv_b.at[t], bsend_sem.at[t], brecv_sem.at[t])
 
         def from_owner(j, _):
@@ -361,11 +377,48 @@
         for g in range(GROUPS):
             freshp[g] = parts(fresh[g * 32 : (g + 1) * 32].reshape(256, W))
     update_cache(STEPS - 1)
-    cache_store = pltpu.make_async_copy(cache, cache_out, out_sem.at[2])
+    cache_store = pltpu.make_async_copy(cache, cache_out, out_sem.at[5])
     cache_store.start()
+    stores.append(cache_store)
+    for store in stores:
+        store.wait()
+
+
+def finish(
+    idx_sm, table_hbm, answers_hbm, cache_hbm, pending_hbm, table_out, cache_out, pending_out,
+    table, answers, cache, pending, in_sem, out_sem,
+):
+    loads = [
+        pltpu.make_async_copy(answers_hbm, answers, in_sem.at[0]),
+        pltpu.make_async_copy(table_hbm, table.at[pl.ds(0, ROWS)], in_sem.at[1]),
+        pltpu.make_async_copy(cache_hbm, cache, in_sem.at[2]),
+        pltpu.make_async_copy(pending_hbm, pending, in_sem.at[3]),
+    ]
+    for load in loads:
+        load.start()
+    loads[2].wait()
+    cache_store = pltpu.make_async_copy(cache, cache_out, out_sem.at[0])
+    cache_store.start()
+    loads[3].wait()
+    pending_store = pltpu.make_async_copy(pending, pending_out, out_sem.at[1])
+    pending_store.start()
+    loads[0].wait()
+    loads[1].wait()
+    for t in range(STEPS):
+
+        def rows_of(src, _):
+            for k in range(CAP):
+                i = idx_sm[src, 0, t * CAP + k]
+                i = jnp.where(i < 0, ROWS, jnp.minimum(i, ROWS))
+                table[pl.ds(i, 1), :] = answers[t, src, k : k + 1, :]
+            return 0
+
+        lax.fori_loop(0, N, rows_of, 0, unroll=2)
+    table_store = pltpu.make_async_copy(table.at[pl.ds(0, ROWS)], table_out, out_sem.at[2])
+    table_store.start()
+    cache_store.wait()
     pending_store.wait()
     table_store.wait()
-    cache_store.wait()
 
 
 def body(table, accum, cache_values, cache_rows, pending, batch_slots, targets, dirty):
@@ -377,16 +430,17 @@
     hbm = pl.BlockSpec(memory_space=pl.ANY)
     dma = pltpu.SemaphoreType.DMA
     tiles = (N, CAP, W)
-    new_table, new_accum, new_cache, new_pending = pl.pallas_call(
+    answers, idx, new_accum, new_cache, new_pending = pl.pallas_call(
         kernel,
         out_shape=(
-            jax.ShapeDtypeStruct((ROWS, W), F32),
+            jax.ShapeDtypeStruct((STEPS, *tiles), F32),
+            jax.ShapeDtypeStruct((N, 1, W), I32),
             jax.ShapeDtypeStruct((64, W), F32),
             jax.ShapeDtypeStruct((SLOTS, W), F32),
             jax.ShapeDtypeStruct((SLOTS, W), F32),
         ),
         in_specs=[smem, vmem, vmem, vmem, vmem, hbm, hbm, hbm, hbm],
-        out_specs=(hbm, vmem, hbm, hbm),
+        out_specs=(hbm, hbm, vmem, hbm, hbm),
         scratch_shapes=[
             pltpu.VMEM((ROWS, W), F32),
             pltpu.VMEM((SLOTS, W), F32),
@@ -411,16 +465,19 @@
             pltpu.VMEM((8, N), I32),
             pltpu.SMEM((8, N), I32),
             pltpu.VMEM((STEPS, GROUPS, 8, 256), I32),
-            pltpu.VMEM((N * CAP, W), I32),
-            pltpu.VMEM((8, N * CAP), I32),
+            pltpu.VMEM((STEPS, N * CAP, W), I32),
+            pltpu.VMEM((STEPS, 8, N * CAP), I32),
             pltpu.VMEM((N * CAP, N * CAP), BF16),
             pltpu.VMEM((N * CAP, W), F32),
-            pltpu.VMEM(tiles, F32),
             pltpu.VMEM((N * CAP, W), F32),
-            pltpu.VMEM((N * CAP, 2 * W), F32),
+            pltpu.VMEM((N * CAP, W), F32),
+            pltpu.VMEM((STEPS, GROUPS, 1024, W), F32),
+            pltpu.VMEM((N * CAP, 2 * W), BF16),
+            pltpu.VMEM((STEPS, N * CAP, 2 * W), BF16),
+            pltpu.VMEM((N * CAP, W), F32),
             dma((4,)),
             dma((2,)),
-            dma((3,)),
+            dma((6,)),
             dma((1,)),
             dma((1,)),
             dma((STEPS,)),
@@ -434,6 +491,24 @@
     )(
         owners, keys, dirty, rows, accum.reshape(64, W), table, cache_values, pending, targets
     )
+    new_table, new_cache, new_pending = pl.pallas_call(
+        finish,
+        out_shape=(
+            jax.ShapeDtypeStruct((ROWS, W), F32),
+            jax.ShapeDtypeStruct((SLOTS, W), F32),
+            jax.ShapeDtypeStruct((SLOTS, W), F32),
+        ),
+        in_specs=[smem, hbm, hbm, hbm, hbm],
+        out_specs=(hbm, hbm, hbm),
+        scratch_shapes=[
+            pltpu.VMEM((ROWS + 8, W), F32),
+            pltpu.VMEM((STEPS, *tiles), F32),
+            pltpu.VMEM((SLOTS, W), F32),
+            pltpu.VMEM((SLOTS, W), F32),
+            dma((4,)),
+            dma((3,)),
+        ],
+    )(idx, table, answers, new_cache, new_pending)
     return new_table, new_accum.reshape(-1), new_cache, new_pending
 
 

time: 145 us -> 122 us (0.84)
  Pallas kernels: 132 us -> 117 us
  local copies, waits for them, and re-layouts: 11.9 us -> 3.64 us
    pallas_call x1 -> x2, Pallas kernels: 132 us -> 117 us  [the longest x1 103 us: body(): pl.pallas_call(kernel, out_shape=(jax.ShapeDtypeStruct((STEPS, *tiles), F...]
    unnamed x13 -> x6, local copies, waits for them, and re-layouts: 10.1 us -> 1.78 us
where the time goes in v2:
time: 122 us
  Pallas kernels  117 us (96%)
  local copies, waits for them, and re-layouts  3.64 us (3%)
    pallas_call x1, Pallas kernels, body(): pl.pallas_call(kernel, out_shape=(jax.ShapeDtypeStruct((STEPS, *tiles), F...  103 us
    pallas_call x1, Pallas kernels, body(): pl.pallas_call(finish, out_shape=(jax.ShapeDtypeStruct((ROWS, W), F32), j...  14.8 us

profile of v2, /device:TPU:1, one launch (start us, length us, event | category | flops | bytes accessed | tf_op | source)
XLA Modules:
  0.0 122.1 jit_solution(15608193313986714959)
XLA Ops:
  0.6 0.8 reshape.20.rows_ref
  1.4 0.0 copy-start
  1.4 0.1 slice_reduce_fusion
  1.5 0.5 and_select_fusion.owner_sm
  2.1 1.2 copy.13
  3.2 1.0 reshape.21.keys_ref
  4.2 0.0 copy-done
  4.2 102.5 %shard_map.111 = (f32[3,128,8,128]{3,2,1,0:T(8,128)}, s32[128,1,128]{2,1,0:T(1,128)}, f32[64,128]{1,0:T(8,128)}, f32[4096,128]{1,0:T(8,128)}, f32[4096,128]{1,0:T(8,128)}) custom-call(s32[128]{0:T(128)} %and_select_fusion.owner_sm, s32[3,32,256]{2,1,0:T(8,128)} %reshape.21.keys_ref, s32[3,512]{1,0:T(4,128)} %dirty_ref.1, s32[128,32]{1,0:T(8,128)} %copy-done, ...), custom_call_target="tpu_custom_call" | custom-call | tf_op jit(solution)/shard_map/pallas_call | solution.py:433
  106.7 0.0 copy-start.1
  106.7 14.8 %shard_map.112 = (f32[8192,128]{1,0:T(8,128)}, f32[4096,128]{1,0:T(8,128)}, f32[4096,128]{1,0:T(8,128)}) custom-call(s32[128,1,128]{2,1,0:T(1,128)} %get-tuple-element.12.idx_sm, f32[8192,128]{1,0:T(8,128)} %table_hbm.3, f32[3,128,8,128]{3,2,1,0:T(8,128)} %get-tuple-element.13.answers_hbm, f32[4096,128]{1,0:T(8,128)} %get-tuple-element.14.cache_hbm, ...), custom_call_target="tpu_custom_call" | custom-call | tf_op jit(solution)/shard_map/pallas_call | solution.py:494
  121.5 0.0 copy-done.1
  121.5 0.6 copy.15
Async XLA Ops:
  1.4 2.8 %copy-start = (s32[128,32]{1,0:T(8,128)}, s32[128,32]{1,0:T(8,128)S(1)}, u32[]{:S(2)}) copy-start(s32[128,32]{1,0:T(8,128)S(1)} %reshape.20.rows_ref) | copy-start | bytes 49156
  106.7 14.8 %copy-start.1 = (f32[64,128]{1,0:T(8,128)S(1)}, f32[64,128]{1,0:T(8,128)}, u32[]{:S(2)}) copy-start(f32[64,128]{1,0:T(8,128)} %get-tuple-element.17) | copy-start | bytes 98308

commit v3 on v2

--- a/solution.py
+++ b/solution.py
@@ -8,6 +8,7 @@
 from jax.sharding import PartitionSpec as P
 
 LEARN_RATE = 0.3
+FAR_A, FAR_B, FAR_M = 6, 2, 9
 LOGICAL = pl.DeviceIdType.LOGICAL
 F32, BF16, I32 = jnp.float32, jnp.bfloat16, jnp.int32
 
@@ -57,20 +58,34 @@
 
 
 def kernel(
-    owner_sm, keys_ref, dirty_ref, rows_ref, accum_ref, table_hbm, cache_hbm, pending_hbm, targets_hbm,
+    held_sm, keys_ref, dirty_ref, rows_ref, accum_ref, table_hbm, cache_hbm, pending_hbm, targets_hbm,
     answers_out, idx_out, accum_out, cache_out, pending_out,
     table, cache, waiting, targets, counts, sel, mix, pick, base, flush, fresh, freshp, bag_grad,
     send_f, recv_f, send_b, recv_b, idx_send, idx_recv, idx_sm, inv_v, inv_sm,
-    place, ycol, yrow, same, share, old, acc_old, gone, gotp, deltap, more,
+    place, placec, ycol, yrow, same, share, old, acc_old, gone, gotp, deltap, more,
     in_sem, sm_sem, out_sem, isend_sem, irecv_sem, fsend_sem, frecv_sem, bsend_sem, brecv_sem,
 ):
     gx, gy = lax.axis_index("gx"), lax.axis_index("gy")
     me = gx * 16 + gy
 
-    quarter, inner_id = me // 32, lax.rem(me, 32)
-
-    def partner(q, k):
-        return lax.rem(quarter + q, 4) * 32 + lax.rem(inner_id + k, 32)
+    quarter, core, px, py = gx // 2, lax.rem(gx, 2), gy // 4, lax.rem(gy, 4)
+    far = (2, 1, 3, 0)
+    line = [lax.rem(core + 1 - c, 2) * 16 + lax.rem(py + dy, 4) for dy in far for c in range(2)]
+
+    def each_partner(q, act):
+        plane = lax.rem(quarter + q, 4) * 32
+
+        def row(n, _):
+            dx = lax.rem(FAR_A * n * n + FAR_B * n + 2, FAR_M)
+            start = plane + lax.rem(px + dx, 4) * 4
+            for p in line:
+                act(start + p)
+            return 0
+
+        lax.fori_loop(0, 4 if q else 3, row, 0)
+        if q == 0:
+            for p in line[:-1]:
+                act(plane + px * 4 + p)
 
     loads = [
         pltpu.make_async_copy(cache_hbm, cache, in_sem.at[0]),
@@ -82,13 +97,8 @@
         load.start()
     barrier = pltpu.get_barrier_semaphore()
 
-    for q in range(4):
-
-        def greet(k, _):
-            pl.semaphore_signal(barrier, inc=1, device_id=partner(q, k), device_id_type=LOGICAL)
-            return 0
-
-        lax.fori_loop(0 if q else 1, 32, greet, 0)
+    for q in far:
+        each_partner(q, lambda p: pl.semaphore_signal(barrier, inc=1, device_id=p, device_id_type=LOGICAL))
 
     lane_i = iota((BLOCK, 256), 1)
     sub_i = iota((BLOCK, 256), 0)
@@ -125,7 +135,7 @@
     sent_found = dot_tn(perm, exact_bf16(found))
     sent_hi = dot_tn(perm, exact_bf16(at_hi))
     sent_lo = dot_tn(perm, exact_bf16(at_lo))
-    sent = jnp.where(sent_found > 0.5, sent_hi * 128.0 + sent_lo, -1.0).astype(I32)
+    sent = jnp.where(sent_found > 0.5, sent_hi * 128.0 + sent_lo, float(ROWS)).astype(I32)
     idx_send[...] = sent.reshape(N, 1, W)
     block_row = exact_bf16(iota((8, N), 1).astype(F32))
     inv_v[...] = jnp.minimum(dot(block_row, perm), N - 1.0).astype(I32)
@@ -142,6 +152,9 @@
             inside = dot(jnp.ones((8, N), BF16), part)
             offset = (iota((8, 256), 1) // CAP * BLOCK).astype(F32)
             place[t, g] = jnp.where(inside < -0.5, -1.0, inside + offset).astype(I32)
+            inside = dot_tn(part, jnp.ones((N, W), BF16))
+            offset = (iota((256, W), 0) // CAP * BLOCK).astype(F32)
+            placec[t, g] = jnp.where(inside < -0.5, -1.0, inside + offset).astype(I32)
 
     def build_counts(t):
         def group(g, _):
@@ -156,7 +169,7 @@
                 counts[h // 8, pl.ds(row, 16), (h % 8) * 128 : (h % 8 + 1) * 128] = r[h * 16 : (h + 1) * 16]
             return 0
 
-        lax.fori_loop(0, 32, group, 0, unroll=4)
+        lax.fori_loop(0, 32, group, 0, unroll=8)
 
     def build_sel(t):
         def group(g, _):
@@ -165,16 +178,17 @@
             gone[t, g] = dot(s, jnp.ones((256, W), BF16))
             return 0
 
-        lax.fori_loop(0, GROUPS, group, 0)
+        lax.fori_loop(0, GROUPS, group, 0, unroll=2)
 
     def build_flush_plan(t):
         def group(g, _):
             s = sel[t, g]
             mix[g] = dot(counts[g], s).astype(BF16).T
-            base[g] = joined(dot_tn(s, parts(waiting[pl.ds(pl.multiple_of(g * 1024, 1024), 1024), :])))
-            return 0
-
-        lax.fori_loop(0, GROUPS, group, 0)
+            st = one_hot(iota((256, 1024), 1) == placec[t, g, :, :1])
+            base[g] = joined(dot(st, parts(waiting[pl.ds(pl.multiple_of(g * 1024, 1024), 1024), :])))
+            return 0
+
+        lax.fori_loop(0, GROUPS, group, 0, unroll=2)
 
     def pooled_base(masked_by):
         total = jnp.zeros((BAGS, 2 * W), F32)
@@ -190,7 +204,7 @@
             pick[g] = dot(counts[g], sel[t_prev, g]).astype(BF16)
             return 0
 
-        lax.fori_loop(0, GROUPS, group, 0)
+        lax.fori_loop(0, GROUPS, group, 0, unroll=2)
 
     def update_waiting(t):
         def group(g, _):
@@ -199,7 +213,7 @@
             waiting[at, :] = jnp.where(gone[t, g] > 0.5, 0.0, w)
             return 0
 
-        lax.fori_loop(0, GROUPS, group, 0)
+        lax.fori_loop(0, GROUPS, group, 0, unroll=2)
 
     def update_cache(t):
         def group(g, _):
@@ -208,28 +222,26 @@
             cache[at, :] = jnp.where(gone[t, g] > 0.5, new, cache[at, :])
             return 0
 
-        lax.fori_loop(0, GROUPS, group, 0)
+        lax.fori_loop(0, GROUPS, group, 0, unroll=2)
 
     def send_quarter(q, src, dst, send_sem, recv_sem):
-        def one(k, _):
-            p = partner(q, k)
+        def one(p):
             pltpu.make_async_remote_copy(
                 src_ref=src.at[p], dst_ref=dst.at[me], send_sem=send_sem, recv_sem=recv_sem,
                 device_id=p, device_id_type=LOGICAL,
             ).start()
-            return 0
-
-        lax.fori_loop(0 if q else 1, 32, one, 0)
+
+        each_partner(q, one)
 
     def exchange_start(src, dst, send_sem, recv_sem):
-        for q in range(4):
+        for q in far:
             send_quarter(q, src, dst, send_sem, recv_sem)
         dst[me] = src[me]
 
     def exchange_wait(src, dst, send_sem, recv_sem):
         all_of = pltpu.make_async_remote_copy(
             src_ref=src.at[pl.ds(0, N - 1)], dst_ref=dst.at[pl.ds(0, N - 1)], send_sem=send_sem,
-            recv_sem=recv_sem, device_id=partner(0, 1), device_id_type=LOGICAL,
+            recv_sem=recv_sem, device_id=lax.rem(me + 1, N), device_id_type=LOGICAL,
         )
         all_of.wait_send()
         all_of.wait_recv()
@@ -253,7 +265,7 @@
             share[at, :] = 1.0 / dot(m, jnp.ones((1024, W), BF16))
             return 0
 
-        lax.fori_loop(0, 4, chunk, 0)
+        lax.fori_loop(0, 4, chunk, 0, unroll=2)
 
     def plan_values(t):
         yc = ycol[t]
@@ -262,7 +274,7 @@
         got = joined(dot(hot, parts(accum_out[...])))
         got = jnp.where(iota((N * CAP, W), 1) == yc - head * 128, got, 0.0)
         acc = jnp.sum(got, axis=1, keepdims=True)
-        acc_old[...] = jnp.broadcast_to(jnp.where(yc[:, :1] < 0, 1.0, acc), (N * CAP, W))
+        acc_old[...] = jnp.broadcast_to(jnp.where(yc[:, :1] >= ROWS, 1.0, acc), (N * CAP, W))
 
         def fetch(src, _):
             for k in range(CAP):
@@ -270,7 +282,7 @@
                 old[pl.ds(src * CAP + k, 1), :] = table[pl.ds(i, 1), :]
             return 0
 
-        lax.fori_loop(0, N, fetch, 0)
+        lax.fori_loop(0, N, fetch, 0, unroll=4)
         if t > 0:
 
             def correct(c, _):
@@ -282,11 +294,11 @@
                 old[at, :] = old[at, :] - joined(moved)
                 return 0
 
-            lax.fori_loop(0, 4, correct, 0)
+            lax.fori_loop(0, 4, correct, 0, unroll=2)
 
     def owner_update(t):
         gotp[...] = parts(recv_f[t].reshape(N * CAP, W))
-        for q in range(4):
+        for q in far:
             base_src = lax.rem(quarter + q, 4) * 32
             at = pl.ds(pl.multiple_of(base_src * CAP, 256), 256)
             total = joined(dot(same[at, :], gotp[...]))
@@ -319,21 +331,28 @@
     inv_copy.wait()
     for t in range(STEPS):
         if t > 0:
-            pooled = base_pooled
-            for g in range(GROUPS):
-                pooled = pooled + joined(dot(pick[g], freshp[g]))
+            moved = dot(pick[0], freshp[0])
+            for g in range(1, GROUPS):
+                moved = moved + dot(pick[g], freshp[g])
+            pooled = base_pooled + joined(moved)
         grad = (pooled * (1.0 / BAG) - targets[t]) * (1.0 / BAG)
         bag_grad[...] = parts(grad)
         for g in range(GROUPS):
             out = base[g] + joined(dot(mix[g], bag_grad[...]))
             flush[g * 32 : (g + 1) * 32] = out.reshape(32, CAP, W)
 
-        def to_owner(o, _):
-            send_f[t, o] = flush[jnp.clip(inv_sm[0, o], 0, N - 1)]
-            return 0
-
-        lax.fori_loop(0, N, to_owner, 0, unroll=8)
-        exchange_start(send_f.at[t], recv_f.at[t], fsend_sem.at[t], frecv_sem.at[t])
+        for n, q in enumerate((*far, None)):
+            if q is not None:
+                first = lax.rem(quarter + q, 4) * 32
+
+                def to_owner(o, _):
+                    send_f[t, first + o] = flush[jnp.clip(inv_sm[0, first + o], 0, N - 1)]
+                    return 0
+
+                lax.fori_loop(0, 32, to_owner, 0, unroll=8)
+            if n > 0:
+                send_quarter(far[n - 1], send_f.at[t], recv_f.at[t], fsend_sem.at[t], frecv_sem.at[t])
+        recv_f[t, me] = send_f[t, me]
         update_waiting(t)
         if t == STEPS - 1:
             pending_store = pltpu.make_async_copy(waiting, pending_out, out_sem.at[0])
@@ -370,7 +389,7 @@
         exchange_wait(send_b.at[t], recv_b.at[t], bsend_sem.at[t], brecv_sem.at[t])
 
         def from_owner(j, _):
-            fresh[j] = recv_b[t, jnp.clip(owner_sm[j], 0, N - 1)]
+            fresh[j] = recv_b[t, jnp.clip(lax.div(held_sm[j * BLOCK], ROWS), 0, N - 1)]
             return 0
 
         lax.fori_loop(0, N, from_owner, 0, unroll=8)
@@ -408,12 +427,10 @@
 
         def rows_of(src, _):
             for k in range(CAP):
-                i = idx_sm[src, 0, t * CAP + k]
-                i = jnp.where(i < 0, ROWS, jnp.minimum(i, ROWS))
-                table[pl.ds(i, 1), :] = answers[t, src, k : k + 1, :]
-            return 0
-
-        lax.fori_loop(0, N, rows_of, 0, unroll=2)
+                table[pl.ds(idx_sm[src, 0, t * CAP + k], 1), :] = answers[t, src, k : k + 1, :]
+            return 0
+
+        lax.fori_loop(0, N, rows_of, 0, unroll=4)
     table_store = pltpu.make_async_copy(table.at[pl.ds(0, ROWS)], table_out, out_sem.at[2])
     table_store.start()
     cache_store.wait()
@@ -424,7 +441,6 @@
 def body(table, accum, cache_values, cache_rows, pending, batch_slots, targets, dirty):
     keys = batch_slots.reshape(STEPS, 32, 256)
     rows = cache_rows.reshape(N, BLOCK)
-    owners = rows[:, 0] // ROWS
     vmem = pl.BlockSpec(memory_space=pltpu.VMEM)
     smem = pl.BlockSpec(memory_space=pltpu.SMEM)
     hbm = pl.BlockSpec(memory_space=pl.ANY)
@@ -465,6 +481,7 @@
             pltpu.VMEM((8, N), I32),
             pltpu.SMEM((8, N), I32),
             pltpu.VMEM((STEPS, GROUPS, 8, 256), I32),
+            pltpu.VMEM((STEPS, GROUPS, 256, W), I32),
             pltpu.VMEM((STEPS, N * CAP, W), I32),
             pltpu.VMEM((STEPS, 8, N * CAP), I32),
             pltpu.VMEM((N * CAP, N * CAP), BF16),
@@ -489,7 +506,7 @@
             collective_id=0, has_side_effects=True, vmem_limit_bytes=56 * 1024 * 1024
         ),
     )(
-        owners, keys, dirty, rows, accum.reshape(64, W), table, cache_values, pending, targets
+        cache_rows, keys, dirty, rows, accum.reshape(64, W), table, cache_values, pending, targets
     )
     new_table, new_cache, new_pending = pl.pallas_call(
         finish,

time: 122 us -> 106 us (0.87)
  Pallas kernels: 117 us -> 101 us
    pallas_call x1, Pallas kernels: 103 us -> 90.1 us  [body(): pl.pallas_call(kernel, out_shape=(jax.ShapeDtypeStruct((STEPS, *tiles), F...]
    pallas_call x1, Pallas kernels: 14.8 us -> 10.9 us  [body(): pl.pallas_call(finish, out_shape=(jax.ShapeDtypeStruct((ROWS, W), F32), j...]
where the time goes in v3:
time: 106 us
  Pallas kernels  101 us (95%)
  local copies, waits for them, and re-layouts  4.16 us (4%)
    pallas_call x1, Pallas kernels, body(): pl.pallas_call(kernel, out_shape=(jax.ShapeDtypeStruct((STEPS, *tiles), F...  90.1 us
    pallas_call x1, Pallas kernels, body(): pl.pallas_call(finish, out_shape=(jax.ShapeDtypeStruct((ROWS, W), F32), j...  10.9 us

profile of v3, /device:TPU:1, one launch (start us, length us, event | category | flops | bytes accessed | tf_op | source)
XLA Modules:
  0.0 105.8 jit_solution(6610355323446820773)
XLA Ops:
  0.6 1.4 %reshape.21.rows_ref = s32[128,32]{1,0:T(8,128)} reshape(s32[4096]{0:T(1024)} %held_sm.1) | data formatting | bytes 32768 | tf_op jit(solution)/shard_map/reshape | solution.py:443
  2.1 1.2 %copy.13 = s32[3,512,16]{2,1,0:T(8,128)S(1)} copy(s32[3,512,16]{1,2,0:T(8,128)} %param.13) | data formatting | bytes 196608 | tf_op args[5]
  3.2 1.0 reshape.20.keys_ref
  4.2 90.1 %shard_map.111 = (f32[3,128,8,128]{3,2,1,0:T(8,128)}, s32[128,1,128]{2,1,0:T(1,128)}, f32[64,128]{1,0:T(8,128)}, f32[4096,128]{1,0:T(8,128)}, f32[4096,128]{1,0:T(8,128)}) custom-call(s32[4096]{0:T(1024)} %held_sm.1, s32[3,32,256]{2,1,0:T(8,128)} %reshape.20.keys_ref, s32[3,512]{1,0:T(4,128)} %dirty_ref.1, s32[128,32]{1,0:T(8,128)} %reshape.21.rows_ref, ...), custom_call_target="tpu_custom_call" | custom-call | tf_op jit(solution)/shard_map/pallas_call | solution.py:449
  94.3 0.0 copy-start
  94.3 10.9 %shard_map.112 = (f32[8192,128]{1,0:T(8,128)}, f32[4096,128]{1,0:T(8,128)}, f32[4096,128]{1,0:T(8,128)}) custom-call(s32[128,1,128]{2,1,0:T(1,128)} %get-tuple-element.12.idx_sm, f32[8192,128]{1,0:T(8,128)} %table_hbm.3, f32[3,128,8,128]{3,2,1,0:T(8,128)} %get-tuple-element.13.answers_hbm, f32[4096,128]{1,0:T(8,128)} %get-tuple-element.14.cache_hbm, ...), custom_call_target="tpu_custom_call" | custom-call | tf_op jit(solution)/shard_map/pallas_call | solution.py:511
  105.2 0.0 copy-done
  105.2 0.6 copy.15
Async XLA Ops:
  94.3 10.9 %copy-start = (f32[64,128]{1,0:T(8,128)S(1)}, f32[64,128]{1,0:T(8,128)}, u32[]{:S(2)}) copy-start(f32[64,128]{1,0:T(8,128)} %get-tuple-element.17) | copy-start | bytes 98308

commit v4 on v3

--- a/solution.py
+++ b/solution.py
@@ -58,11 +58,11 @@
 
 
 def kernel(
-    held_sm, keys_ref, dirty_ref, rows_ref, accum_ref, table_hbm, cache_hbm, pending_hbm, targets_hbm,
+    held_hbm, keys_ref, dirty_ref, rows_ref, accum_ref, table_hbm, cache_hbm, pending_hbm, targets_hbm,
     answers_out, idx_out, accum_out, cache_out, pending_out,
     table, cache, waiting, targets, counts, sel, mix, pick, base, flush, fresh, freshp, bag_grad,
-    send_f, recv_f, send_b, recv_b, idx_send, idx_recv, idx_sm, inv_v, inv_sm,
-    place, placec, ycol, yrow, same, share, old, acc_old, gone, gotp, deltap, more,
+    send_f, recv_f, send_b, recv_b, idx_send, idx_recv, idx_sm, inv_v, inv_sm, held_sm,
+    in_block, place, placec, ycol, yrow, same, share, old, acc_old, gone, gotp, deltap, more,
     in_sem, sm_sem, out_sem, isend_sem, irecv_sem, fsend_sem, frecv_sem, bsend_sem, brecv_sem,
 ):
     gx, gy = lax.axis_index("gx"), lax.axis_index("gy")
@@ -92,6 +92,7 @@
         pltpu.make_async_copy(targets_hbm, targets, in_sem.at[1]),
         pltpu.make_async_copy(pending_hbm, waiting, in_sem.at[2]),
         pltpu.make_async_copy(table_hbm, table, in_sem.at[3]),
+        pltpu.make_async_copy(held_hbm, held_sm, in_sem.at[4]),
     ]
     for load in loads:
         load.start()
@@ -105,11 +106,20 @@
     before = one_hot(sub_i < lane_i % BLOCK)
     spread = one_hot(sub_i == lane_i % BLOCK)
     rows = rows_ref[...]
-    local = rows - (rows // ROWS) * ROWS
+    owner = rows // ROWS
+    local = rows - owner * ROWS
     local_hi = local // 128
     local_lo = local - local_hi * 128
-    rep_hi = dot(exact_bf16(local_hi.astype(F32)), spread)
-    rep_lo = dot(exact_bf16(local_lo.astype(F32)), spread)
+    lift = one_hot(iota((N, 32), 1) == iota((N, 32), 0) // 4)
+    lane, part_of = iota((N, W), 1), iota((N, W), 0) % 4
+    fold = one_hot(iota((W, 256), 0) % BLOCK == iota((W, 256), 1) % BLOCK)
+
+    def lifted(x, keep):
+        return jnp.where(keep, dot(lift, exact_bf16(x.astype(F32))), 0.0)
+
+    rep_hi = dot(exact_bf16(lifted(local_hi, lane // BLOCK == part_of)), fold)
+    rep_lo = dot(exact_bf16(lifted(local_lo, lane // BLOCK == part_of)), fold)
+    owner_col = jnp.sum(lifted(owner, lane == part_of * BLOCK), axis=1, keepdims=True).astype(I32)
     want = (iota((N, 256), 1) // BLOCK).astype(F32)
     inner = (iota((N, 256), 1) % BLOCK).astype(F32)
     found = jnp.zeros((N, W), F32)
@@ -130,7 +140,6 @@
         at_hi = at_hi + dot(exact_bf16(chosen * rep_hi), gather)
         at_lo = at_lo + dot(exact_bf16(chosen * rep_lo), gather)
         at_in = at_in + dot(exact_bf16(chosen * inner), gather)
-    owner_col = rows[:, :1] // ROWS
     perm = one_hot(owner_col == iota((N, N), 1))
     sent_found = dot_tn(perm, exact_bf16(found))
     sent_hi = dot_tn(perm, exact_bf16(at_hi))
@@ -141,20 +150,7 @@
     inv_v[...] = jnp.minimum(dot(block_row, perm), N - 1.0).astype(I32)
     inv_copy = pltpu.make_async_copy(inv_v, inv_sm, sm_sem.at[0])
     inv_copy.start()
-    in_block = jnp.where(found > 0.5, at_in, -1.0)
-    for t in range(STEPS):
-        rep8 = one_hot(iota((W, 256), 0) == iota((W, 256), 1) % CAP + t * CAP)
-        wide_in = dot(exact_bf16(in_block), rep8)
-        for g in range(GROUPS):
-            jj = iota((N, 256), 0) - g * 32
-            here = jj == iota((N, 256), 1) // CAP
-            part = exact_bf16(jnp.where(here, wide_in, 0.0))
-            inside = dot(jnp.ones((8, N), BF16), part)
-            offset = (iota((8, 256), 1) // CAP * BLOCK).astype(F32)
-            place[t, g] = jnp.where(inside < -0.5, -1.0, inside + offset).astype(I32)
-            inside = dot_tn(part, jnp.ones((N, W), BF16))
-            offset = (iota((256, W), 0) // CAP * BLOCK).astype(F32)
-            placec[t, g] = jnp.where(inside < -0.5, -1.0, inside + offset).astype(I32)
+    in_block[...] = jnp.where(found > 0.5, at_in, -1.0)
 
     def build_counts(t):
         def group(g, _):
@@ -171,9 +167,25 @@
 
         lax.fori_loop(0, 32, group, 0, unroll=8)
 
+    def build_place(t):
+        rep8 = one_hot(iota((W, 256), 0) == iota((W, 256), 1) % CAP + t * CAP)
+        wide_in = dot(exact_bf16(in_block[...]), rep8)
+        for g in range(GROUPS):
+            jj = iota((N, 256), 0) - g * 32
+            here = jj == iota((N, 256), 1) // CAP
+            part = exact_bf16(jnp.where(here, wide_in, 0.0))
+            inside = dot(jnp.ones((8, N), BF16), part)
+            offset = (iota((8, 256), 1) // CAP * BLOCK).astype(F32)
+            place[g] = jnp.where(inside < -0.5, -1.0, inside + offset).astype(I32)
+            inside = dot_tn(part, jnp.ones((N, W), BF16))
+            offset = (iota((256, W), 0) // CAP * BLOCK).astype(F32)
+            placec[g] = jnp.where(inside < -0.5, -1.0, inside + offset).astype(I32)
+
     def build_sel(t):
+        build_place(t)
+
         def group(g, _):
-            s = one_hot(iota((1024, 256), 0) == place[t, g, :1, :])
+            s = one_hot(iota((1024, 256), 0) == place[g, :1, :])
             sel[t, g] = s
             gone[t, g] = dot(s, jnp.ones((256, W), BF16))
             return 0
@@ -184,7 +196,7 @@
         def group(g, _):
             s = sel[t, g]
             mix[g] = dot(counts[g], s).astype(BF16).T
-            st = one_hot(iota((256, 1024), 1) == placec[t, g, :, :1])
+            st = one_hot(iota((256, 1024), 1) == placec[g, :, :1])
             base[g] = joined(dot(st, parts(waiting[pl.ds(pl.multiple_of(g * 1024, 1024), 1024), :])))
             return 0
 
@@ -364,6 +376,7 @@
             idx_copy.start()
             plan_rows(0)
             loads[3].wait()
+            loads[4].wait()
             idx_copy.wait()
         plan_values(t)
         if t > 0:
@@ -404,25 +417,26 @@
 
 
 def finish(
-    idx_sm, table_hbm, answers_hbm, cache_hbm, pending_hbm, table_out, cache_out, pending_out,
-    table, answers, cache, pending, in_sem, out_sem,
+    idx_hbm, accum_in, table_hbm, answers_hbm, cache_hbm, pending_hbm,
+    accum_out, table_out, cache_out, pending_out,
+    table, answers, cache, pending, idx_sm, in_sem, out_sem,
 ):
     loads = [
         pltpu.make_async_copy(answers_hbm, answers, in_sem.at[0]),
         pltpu.make_async_copy(table_hbm, table.at[pl.ds(0, ROWS)], in_sem.at[1]),
         pltpu.make_async_copy(cache_hbm, cache, in_sem.at[2]),
         pltpu.make_async_copy(pending_hbm, pending, in_sem.at[3]),
+        pltpu.make_async_copy(idx_hbm, idx_sm, in_sem.at[4]),
     ]
-    for load in loads:
-        load.start()
-    loads[2].wait()
-    cache_store = pltpu.make_async_copy(cache, cache_out, out_sem.at[0])
-    cache_store.start()
-    loads[3].wait()
-    pending_store = pltpu.make_async_copy(pending, pending_out, out_sem.at[1])
-    pending_store.start()
+    loads[4].start()
+    loads[0].start()
+    loads[1].start()
+    accum_out[...] = accum_in[...]
     loads[0].wait()
     loads[1].wait()
+    loads[2].start()
+    loads[3].start()
+    loads[4].wait()
     for t in range(STEPS):
 
         def rows_of(src, _):
@@ -431,6 +445,13 @@
             return 0
 
         lax.fori_loop(0, N, rows_of, 0, unroll=4)
+        if t == 0:
+            loads[2].wait()
+            cache_store = pltpu.make_async_copy(cache, cache_out, out_sem.at[0])
+            cache_store.start()
+            loads[3].wait()
+            pending_store = pltpu.make_async_copy(pending, pending_out, out_sem.at[1])
+            pending_store.start()
     table_store = pltpu.make_async_copy(table.at[pl.ds(0, ROWS)], table_out, out_sem.at[2])
     table_store.start()
     cache_store.wait()
@@ -440,9 +461,8 @@
 
 def body(table, accum, cache_values, cache_rows, pending, batch_slots, targets, dirty):
     keys = batch_slots.reshape(STEPS, 32, 256)
-    rows = cache_rows.reshape(N, BLOCK)
+    rows = cache_rows.reshape(32, 128)
     vmem = pl.BlockSpec(memory_space=pltpu.VMEM)
-    smem = pl.BlockSpec(memory_space=pltpu.SMEM)
     hbm = pl.BlockSpec(memory_space=pl.ANY)
     dma = pltpu.SemaphoreType.DMA
     tiles = (N, CAP, W)
@@ -455,7 +475,7 @@
             jax.ShapeDtypeStruct((SLOTS, W), F32),
             jax.ShapeDtypeStruct((SLOTS, W), F32),
         ),
-        in_specs=[smem, vmem, vmem, vmem, vmem, hbm, hbm, hbm, hbm],
+        in_specs=[hbm, vmem, vmem, vmem, vmem, hbm, hbm, hbm, hbm],
         out_specs=(hbm, hbm, vmem, hbm, hbm),
         scratch_shapes=[
             pltpu.VMEM((ROWS, W), F32),
@@ -480,8 +500,10 @@
             pltpu.SMEM((N, 1, W), I32),
             pltpu.VMEM((8, N), I32),
             pltpu.SMEM((8, N), I32),
-            pltpu.VMEM((STEPS, GROUPS, 8, 256), I32),
-            pltpu.VMEM((STEPS, GROUPS, 256, W), I32),
+            pltpu.SMEM((SLOTS,), I32),
+            pltpu.VMEM((N, W), F32),
+            pltpu.VMEM((GROUPS, 8, 256), I32),
+            pltpu.VMEM((GROUPS, 256, W), I32),
             pltpu.VMEM((STEPS, N * CAP, W), I32),
             pltpu.VMEM((STEPS, 8, N * CAP), I32),
             pltpu.VMEM((N * CAP, N * CAP), BF16),
@@ -492,7 +514,7 @@
             pltpu.VMEM((N * CAP, 2 * W), BF16),
             pltpu.VMEM((STEPS, N * CAP, 2 * W), BF16),
             pltpu.VMEM((N * CAP, W), F32),
-            dma((4,)),
+            dma((5,)),
             dma((2,)),
             dma((6,)),
             dma((1,)),
@@ -508,24 +530,26 @@
     )(
         cache_rows, keys, dirty, rows, accum.reshape(64, W), table, cache_values, pending, targets
     )
-    new_table, new_cache, new_pending = pl.pallas_call(
+    new_accum, new_table, new_cache, new_pending = pl.pallas_call(
         finish,
         out_shape=(
+            jax.ShapeDtypeStruct((64, W), F32),
             jax.ShapeDtypeStruct((ROWS, W), F32),
             jax.ShapeDtypeStruct((SLOTS, W), F32),
             jax.ShapeDtypeStruct((SLOTS, W), F32),
         ),
-        in_specs=[smem, hbm, hbm, hbm, hbm],
-        out_specs=(hbm, hbm, hbm),
+        in_specs=[hbm, vmem, hbm, hbm, hbm, hbm],
+        out_specs=(vmem, hbm, hbm, hbm),
         scratch_shapes=[
             pltpu.VMEM((ROWS + 8, W), F32),
             pltpu.VMEM((STEPS, *tiles), F32),
             pltpu.VMEM((SLOTS, W), F32),
             pltpu.VMEM((SLOTS, W), F32),
-            dma((4,)),
+            pltpu.SMEM((N, 1, W), I32),
+            dma((5,)),
             dma((3,)),
         ],
-    )(idx, table, answers, new_cache, new_pending)
+    )(idx, new_accum, table, answers, new_cache, new_pending)
     return new_table, new_accum.reshape(-1), new_cache, new_pending
 
 

time: 106 us -> 104 us (0.981)
  local copies, waits for them, and re-layouts: 4.16 us -> 2.12 us
    reshape x1 -> x0, local copies, waits for them, and re-layouts: 1.43 us -> none  [body(): rows = cache_rows.reshape(N, BLOCK)]
where the time goes in v4:
time: 104 us
  Pallas kernels  101 us (97%)
  local copies, waits for them, and re-layouts  2.12 us (2%)
    pallas_call x1, Pallas kernels, body(): pl.pallas_call(kernel, out_shape=(jax.ShapeDtypeStruct((STEPS, *tiles), F...  90.3 us
    pallas_call x1, Pallas kernels, body(): pl.pallas_call(finish, out_shape=(jax.ShapeDtypeStruct((64, W), F32), jax...  10.4 us

profile of v4, /device:TPU:1, one launch (start us, length us, event | category | flops | bytes accessed | tf_op | source)
XLA Modules:
  0.0 103.7 jit_solution(2526496033610580613)
XLA Ops:
  0.6 1.2 %copy.13 = s32[3,512,16]{2,1,0:T(8,128)S(1)} copy(s32[3,512,16]{1,2,0:T(8,128)} %param.13) | data formatting | bytes 196608 | tf_op args[5]
  1.8 1.0 reshape.20.keys_ref
  2.8 90.3 %shard_map.111 = (f32[3,128,8,128]{3,2,1,0:T(8,128)}, s32[128,1,128]{2,1,0:T(1,128)}, f32[64,128]{1,0:T(8,128)}, f32[4096,128]{1,0:T(8,128)}, f32[4096,128]{1,0:T(8,128)}) custom-call(s32[4096]{0:T(1024)} %held_hbm.1, s32[3,32,256]{2,1,0:T(8,128)} %reshape.20.keys_ref, s32[3,512]{1,0:T(4,128)} %dirty_ref.1, s32[32,128]{1,0:T(8,128)} %bitcast.3, ...), custom_call_target="tpu_custom_call" | custom-call | tf_op jit(solution)/shard_map/pallas_call | solution.py:469
  93.1 10.4 %shard_map.112 = (f32[64,128]{1,0:T(8,128)}, f32[8192,128]{1,0:T(8,128)}, f32[4096,128]{1,0:T(8,128)}, f32[4096,128]{1,0:T(8,128)}) custom-call(s32[128,1,128]{2,1,0:T(1,128)} %get-tuple-element.13.idx_hbm, f32[64,128]{1,0:T(8,128)} %get-tuple-element.14.accum_in, f32[8192,128]{1,0:T(8,128)} %table_hbm.3, f32[3,128,8,128]{3,2,1,0:T(8,128)} %get-tuple-element.15.answers_hbm, ...), custom_call_target="tpu_custom_call" | custom-call | tf_op jit(solution)/shard_map/pallas_call | solution.py:533

commit v5 on v4

--- a/solution.py
+++ b/solution.py
@@ -429,13 +429,11 @@
         pltpu.make_async_copy(idx_hbm, idx_sm, in_sem.at[4]),
     ]
     loads[4].start()
-    loads[0].start()
-    loads[1].start()
+    for load in loads[:4]:
+        load.start()
     accum_out[...] = accum_in[...]
     loads[0].wait()
     loads[1].wait()
-    loads[2].start()
-    loads[3].start()
     loads[4].wait()
     for t in range(STEPS):
 

time: 104 us -> 103 us (level)
  Pallas kernels: 101 us -> 99.8 us
where the time goes in v5:
time: 103 us
  Pallas kernels  99.8 us (97%)
  local copies, waits for them, and re-layouts  2.12 us (2%)
    pallas_call x1, Pallas kernels, body(): pl.pallas_call(kernel, out_shape=(jax.ShapeDtypeStruct((STEPS, *tiles), F...  90.3 us
    pallas_call x1, Pallas kernels, body(): pl.pallas_call(finish, out_shape=(jax.ShapeDtypeStruct((64, W), F32), jax...  9.44 us

profile of v5, /device:TPU:1, one launch (start us, length us, event | category | flops | bytes accessed | tf_op | source)
XLA Modules:
  0.0 102.7 jit_solution(8499829179924062184)
XLA Ops:
  0.6 1.2 %copy.13 = s32[3,512,16]{2,1,0:T(8,128)S(1)} copy(s32[3,512,16]{1,2,0:T(8,128)} %param.13) | data formatting | bytes 196608 | tf_op args[5]
  1.8 1.0 reshape.20.keys_ref
  2.8 90.3 %shard_map.111 = (f32[3,128,8,128]{3,2,1,0:T(8,128)}, s32[128,1,128]{2,1,0:T(1,128)}, f32[64,128]{1,0:T(8,128)}, f32[4096,128]{1,0:T(8,128)}, f32[4096,128]{1,0:T(8,128)}) custom-call(s32[4096]{0:T(1024)} %held_hbm.1, s32[3,32,256]{2,1,0:T(8,128)} %reshape.20.keys_ref, s32[3,512]{1,0:T(4,128)} %dirty_ref.1, s32[32,128]{1,0:T(8,128)} %bitcast.3, ...), custom_call_target="tpu_custom_call" | custom-call | tf_op jit(solution)/shard_map/pallas_call | solution.py:467
  93.1 9.4 %shard_map.112 = (f32[64,128]{1,0:T(8,128)}, f32[8192,128]{1,0:T(8,128)}, f32[4096,128]{1,0:T(8,128)}, f32[4096,128]{1,0:T(8,128)}) custom-call(s32[128,1,128]{2,1,0:T(1,128)} %get-tuple-element.13.idx_hbm, f32[64,128]{1,0:T(8,128)} %get-tuple-element.14.accum_in, f32[8192,128]{1,0:T(8,128)} %table_hbm.3, f32[3,128,8,128]{3,2,1,0:T(8,128)} %get-tuple-element.15.answers_hbm, ...), custom_call_target="tpu_custom_call" | custom-call | tf_op jit(solution)/shard_map/pallas_call | solution.py:531
